TPU v7x, 32 devices: a whole 2x2x4 slice. The times are simulated.
32 devices in a mesh: rep: 2 (over x), dp: 4 (over z), sp: 4 (over y, core).
Axes of the slice: x: 2, y: 2, z: 4, core: 2. Of those that a mesh axis runs over, the one named last changes fastest.
Arguments:
- hidden: bfloat16 [256, 3584], P(('rep', 'dp')), parts along dimension 0
- w_query: bfloat16 [3584, 3584], replicated
- w_key: bfloat16 [3584, 512], replicated
- w_value: bfloat16 [3584, 512], replicated
- w_out: bfloat16 [3584, 3584], P('sp')
- k_cache: bfloat16 [256, 1024, 4, 128], P(('rep', 'dp'), 'sp'), parts along dimension 0
- v_cache: bfloat16 [256, 1024, 4, 128], P(('rep', 'dp'), 'sp'), parts along dimension 0
- write_pos: int32 [256], P(('rep', 'dp')), parts along dimension 0
- valid_len: int32 [256], P(('rep', 'dp')), parts along dimension 0
Outputs:
- output 1: bfloat16 [256, 3584], P(('rep', 'dp')), parts along dimension 0
- output 2: bfloat16 [256, 1024, 4, 128], P(('rep', 'dp'), 'sp'), parts along dimension 0
- output 3: bfloat16 [256, 1024, 4, 128], P(('rep', 'dp'), 'sp'), parts along dimension 0
There are 2 independent parts. A program takes and returns all parts, laid end to end along the dimension named above; an argument that names none is the same for every part.
All inputs are finite; a program needn't handle non-finite values.
Results may differ from a plain program's by a relative error of at most 0.00655233.
Values are sent between devices in bfloat16 or wider.
A program may use at most 1 GiB of HBM per device.

v0:
```python
import jax
import jax.numpy as jnp
from jax import lax
from jax.sharding import PartitionSpec as P

NEG_FLOOR = -1e30


def solution(mesh):
    row_spec = P(('rep', 'dp'), None)
    cache_spec = P(('rep', 'dp'), 'sp', None, None)
    len_spec = P(('rep', 'dp'))

    def local_step(hidden, w_query, w_key, w_value, w_out, k_cache, v_cache, write_pos, valid_len):
        num_rows, seq_local, kv_heads, head_dim = k_cache.shape
        num_heads = w_query.shape[1] // head_dim
        group_size = num_heads // kv_heads
        shard_idx = lax.axis_index('sp')
        query = jnp.dot(hidden, w_query, preferred_element_type=jnp.float32).astype(jnp.bfloat16)
        query = query.reshape(num_rows, kv_heads, group_size, head_dim)
        key_new = jnp.dot(hidden, w_key, preferred_element_type=jnp.float32).astype(jnp.bfloat16)
        value_new = jnp.dot(hidden, w_value, preferred_element_type=jnp.float32).astype(jnp.bfloat16)
        positions = shard_idx * seq_local + jnp.arange(seq_local, dtype=jnp.int32)
        at_pos = (positions[None, :] == write_pos[:, None])[:, :, None, None]
        k_next = jnp.where(at_pos, key_new.reshape(num_rows, 1, kv_heads, head_dim), k_cache)
        v_next = jnp.where(at_pos, value_new.reshape(num_rows, 1, kv_heads, head_dim), v_cache)
        scores = jnp.einsum('bkgd,bskd->bkgs', query, k_next, preferred_element_type=jnp.float32) * head_dim ** -0.5
        valid_mask = (positions[None, :] < valid_len[:, None])[:, None, None, :]
        scores = jnp.where(valid_mask, scores, -jnp.inf)
        local_max = jnp.maximum(jnp.max(scores, axis=-1), NEG_FLOOR)
        weights = jnp.exp(scores - local_max[..., None])
        local_sum = jnp.sum(weights, axis=-1)
        local_acc = jnp.einsum('bkgs,bskd->bkgd', weights.astype(jnp.bfloat16), v_next, preferred_element_type=jnp.float32)
        global_max = lax.pmax(local_max, 'sp')
        rescale = jnp.exp(local_max - global_max)
        packed = jnp.concatenate([local_acc * rescale[..., None], (local_sum * rescale)[..., None]], axis=-1)
        packed = lax.psum(packed, 'sp')
        attention = (packed[..., :head_dim] / packed[..., head_dim:]).astype(jnp.bfloat16)
        attention = attention.reshape(num_rows, num_heads * head_dim)
        out_rows = w_out.shape[0]
        attn_mine = lax.dynamic_slice_in_dim(attention, shard_idx * out_rows, out_rows, axis=1)
        partial_out = jnp.dot(attn_mine, w_out, preferred_element_type=jnp.float32)
        attn_out = lax.psum(partial_out, 'sp').astype(jnp.bfloat16)
        return attn_out, k_next, v_next

    return jax.shard_map(local_step, mesh=mesh, in_specs=(row_spec, P(), P(), P(), P('sp', None), cache_spec, cache_spec, len_spec, len_spec), out_specs=(row_spec, cache_spec, cache_spec), check_vma=False)
```

profile of v0, /device:TPU:0, one launch (start us, length us, event | category | flops | bytes accessed | tf_op | source)
XLA Modules:
  0.0 132.0 jit_solution(8374100842483825567)
XLA Ops:
  7.2 0.0 copy-start
  7.2 0.0 all-reduce.3.cloned.1.call-start
  7.2 0.9 copy-done
  8.1 2.8 %convolution_convert_fusion.2 = bf16[32,512]{1,0:T(8,128)(2,1)S(1)} fusion(bf16[32,3584]{1,0:T(8,128)(2,1)S(1)} %copy-done, bf16[3584,512]{1,0:T(8,128)(2,1)} %param.11), kind=kOutput, calls=%fused_computation.11 | convolution fusion | flops 117456896 | bytes 3932160 | tf_op jit(solution)/shard_map/dot_general | solution.py:21
  10.9 2.8 %convolution_convert_fusion.1 = bf16[32,512]{1,0:T(8,128)(2,1)S(1)} fusion(bf16[32,3584]{1,0:T(8,128)(2,1)S(1)} %copy-done, bf16[3584,512]{1,0:T(8,128)(2,1)} %param.12), kind=kOutput, calls=%fused_computation.10 | convolution fusion | flops 117456896 | bytes 3932160 | tf_op jit(solution)/shard_map/dot_general | solution.py:22
  13.7 0.0 copy-start.3
  13.7 0.0 copy-start.4
  13.7 10.6 %convolution_convert_fusion = bf16[32,3584]{1,0:T(8,128)(2,1)S(1)} fusion(bf16[32,3584]{1,0:T(8,128)(2,1)S(1)} %copy-done, bf16[3584,3584]{1,0:T(8,128)(2,1)} %param.10), kind=kOutput, calls=%fused_computation.6 | convolution fusion | flops 822198272 | bytes 26148864 | tf_op jit(solution)/shard_map/dot_general | solution.py:19
  24.4 0.3 reshape.75
  24.7 0.0 copy-done.3
  24.7 0.0 copy-done.4
  24.7 0.1 broadcast_compare_fusion.1
  24.8 13.7 %broadcast_select_fusion = (bf16[32,256,4,128]{3,2,1,0:T(4,128)(2,1)}, bf16[32,256,4,128]{3,2,1,0:T(4,128)(2,1)S(1)}) fusion(bf16[32,256,4,128]{3,2,1,0:T(4,128)(2,1)} %param.15, pred[32,256]{1,0:T(8,128)(4,1)S(1)} %get-tuple-element.8, bf16[32,4,128]{2,1,0:T(4,128)(2,1)S(1)} %broadcast_in_dim.56, bf16[32,256,4,128]{3,2,1,0:T(4,128)(2,1)} %param.14, ...), kind=kLoop, calls=%fused_computation.4 | loop fusion | flops 8388608 | bytes 33628160 | tf_op jit(solution)/shard_map/jit(_where)/select_n | solution.py:26
  38.5 0.0 copy-start.2
  38.5 3.4 %copy-done.2 = bf16[32,256,4,128]{3,2,1,0:T(4,128)(2,1)} copy-done((bf16[32,256,4,128]{3,2,1,0:T(4,128)(2,1)}, bf16[32,256,4,128]{3,2,1,0:T(4,128)(2,1)S(1)}, u32[]{:S(2)}) %copy-start.2) | copy-done | bytes 8388632
  41.9 2.4 %fusion.21 = (f32[32,4,7]{2,1,0:T(4,128)S(1)}, f32[32,4,7,256]{3,2,1,0:T(8,128)S(1)}) fusion(bf16[32,4,7,128]{3,2,1,0:T(8,128)(2,1)S(1)} %reshape.75, bf16[32,256,4,128]{3,2,1,0:T(4,128)(2,1)S(1)} %get-tuple-element.6, pred[32,256]{1,0:T(8,128)(4,1)S(1)} %get-tuple-element.7), kind=kOutput, calls=%fused_computation.28 | convolution fusion | flops 59407488 | bytes 9547264 | tf_op jit(solution)/shard_map/bkgd,bskd->bkgs/dot_general | solution.py:27
  44.3 13.5 %pmax.7 = f32[32,4,7]{2,1,0:T(4,128)S(1)} all-reduce(f32[32,4,7]{2,1,0:T(4,128)S(1)} %broadcast_maximum_fusion), channel_id=1, replica_groups=mesh['rep'=2,'dp'=4,'sp'=4] {'sp'}, use_global_device_ids=true, to_apply=%region_1.2 | all-reduce | flops 896 | bytes 7168 | tf_op jit(solution)/shard_map/pmax | solution.py:34
  57.8 0.5 fusion.13
  58.3 0.9 copy.24
  59.2 0.0 copy-start.1
  59.2 4.7 %fusion.10 = f32[32,4,7,128]{3,2,1,0:T(8,128)S(1)} fusion(bf16[32,256,4,128]{3,2,1,0:T(4,128)(2,1)} %get-tuple-element.5, f32[32,4,7,256]{3,2,1,0:T(8,128)S(1)} %get-tuple-element.10, f32[32,4,7]{2,1,0:T(4,128)S(1)} %broadcast_maximum_fusion, f32[32,4,7]{2,1,0:T(4,128)S(1)} %get-tuple-element.4), kind=kOutput, calls=%fused_computation.9 | convolution fusion | flops 59293696 | bytes 9772032 | tf_op jit(solution)/shard_map/bkgs,bskd->bkgd/dot_general | solution.py:33
  64.0 1.2 pad_maximum_fusion
  65.1 0.0 all-reduce.3.cloned.1.call-update
  65.2 36.8 %all-reduce.3.cloned.1.call-done = f32[32,4,7,129]{3,2,1,0:T(8,128)} async-done(((f32[32,4,7,129]{3,2,1,0:T(8,128)}), f32[32,4,7,129]{3,2,1,0:T(8,128)}) %all-reduce.3.cloned.1.call-update) | async-done | bytes 462352 | tf_op jit(solution)/shard_map/psum | solution.py:37
  102.0 1.1 slice.9
  103.0 0.9 copy.29
  103.9 1.3 fusion.16
  105.2 0.3 reshape.76
  105.5 4.0 %fusion.18 = f32[32,3584]{1,0:T(8,128)S(1)} fusion(bf16[896,3584]{1,0:T(8,128)(2,1)} %param.13, bf16[32,3584]{1,0:T(8,128)(2,1)S(1)} %reshape.76, s32[]{:T(128)S(6)} %select_n.17), kind=kOutput, calls=%fused_computation.21 | convolution fusion | flops 205520896 | bytes 6938628 | tf_op jit(solution)/shard_map/dot_general | solution.py:42
  109.5 15.7 %all-reduce.4 = bf16[32,3584]{1,0:T(8,128)(2,1)} all-reduce(f32[32,3584]{1,0:T(8,128)S(1)} %fusion.18), channel_id=1, replica_groups=mesh['rep'=2,'dp'=4,'sp'=4] {'sp'}, use_global_device_ids=true, to_apply=%region_4.5 | all-reduce | flops 114688 | bytes 688128 | tf_op jit(solution)/shard_map/psum | solution.py:43
  125.2 0.0 copy-done.1
  (5 shorter events, 0.1 us)
Async XLA Ops:
  7.2 0.9 copy-start
  7.2 94.8 %all-reduce.3.cloned.1.call-start = ((), (), s32[]{:S(2)}) async-start(), calls=%async_computation | async-start | bytes 2097152 | tf_op jit(solution)/shard_map/psum | solution.py:37
  13.7 11.0 %copy-start.3 = (s32[32]{0:T(128)S(1)}, s32[32]{0:T(128)}, u32[]{:S(2)}) copy-start(s32[32]{0:T(128)} %param.17) | copy-start | bytes 388
  13.7 11.0 %copy-start.4 = (s32[32]{0:T(128)S(1)}, s32[32]{0:T(128)}, u32[]{:S(2)}) copy-start(s32[32]{0:T(128)} %param.16) | copy-start | bytes 388
  38.5 3.4 %copy-start.2 = (bf16[32,256,4,128]{3,2,1,0:T(4,128)(2,1)}, bf16[32,256,4,128]{3,2,1,0:T(4,128)(2,1)S(1)}, u32[]{:S(2)}) copy-start(bf16[32,256,4,128]{3,2,1,0:T(4,128)(2,1)S(1)} %get-tuple-element.6) | copy-start | bytes 25165828
  59.2 66.0 %copy-start.1 = (bf16[32,3584]{1,0:T(8,128)(2,1)S(1)}, bf16[32,3584]{1,0:T(8,128)(2,1)}, u32[]{:S(2)}) copy-start(bf16[32,3584]{1,0:T(8,128)(2,1)} %param.9) | copy-start | bytes 688132
Sparse Core Ops, SparseCore 0:
  65.3 36.6 all-reduce.2
where the time goes:
time: 132 us
  waiting for transfers between devices  36.8 us (28%)
  blocking collectives  29.2 us (22%)
  matrix products  27.3 us (21%)
  other arithmetic  16.8 us (13%)
  between operations  14.2 us (11%)
  local copies, waits for them, and re-layouts  7.75 us (6%)
    psum x1, waiting for transfers between devices, local_step(): packed = lax.psum(packed, 'sp')  36.8 us
    psum x1, blocking collectives, local_step(): attn_out = lax.psum(partial_out, 'sp').astype(jnp.bfloat16)  15.7 us
    select_n x1, other arithmetic, local_step(): jnp.where(at_pos, value_new.reshape(num_rows, 1, kv_heads, head_dim), v_c...  13.7 us
    pmax x1, blocking collectives, local_step(): global_max = lax.pmax(local_max, 'sp')  13.5 us
    dot_general x1, matrix products, local_step(): jnp.dot(hidden, w_query, preferred_element_type=jnp.float32)  10.6 us
    dot_general x1, matrix products, local_step(): jnp.einsum('bkgs,bskd->bkgd', weights.astype(jnp.bfloat16), v_next, prefe...  4.73 us
    unnamed x10, local copies, waits for them, and re-layouts  4.29 us
    dot_general x1, matrix products, local_step(): partial_out = jnp.dot(attn_mine, w_out, preferred_element_type=jnp.float32)  4.02 us
  transfers between devices with their start and end apart: 1, of which 1 were waited for; matrix products, arithmetic and copies ran while one was open for 0% of the time, Pallas kernels for 0%

commit v1 on v0

v1 whole, which is shorter than its diff:
```python
import jax
import jax.numpy as jnp
from jax import lax
from jax.experimental import pallas as pl
from jax.experimental.pallas import tpu as pltpu
from jax.sharding import PartitionSpec as P

MESH = pl.DeviceIdType.MESH
LOG2E = 1.4426950408889634
NSP = 4
ROWS = 32
DIM = 3584
HEAD = 128
KVH = 4
GRP = 7
SEQ = 256
FLAT = SEQ * KVH
QW = GRP * HEAD
PW = QW + 2 * HEAD
NW = 7
WC = DIM // NW
NB = 4
BC = ROWS // NB
HALF = DIM // 2
NE = 4
NC = 2
CC = HALF // NC


def greet(me):
    barrier = pltpu.get_barrier_semaphore()
    for d in range(1, NSP):
        pl.semaphore_signal(barrier, inc=1, device_id={"sp": lax.rem(me + d, NSP)}, device_id_type=MESH)
    pl.semaphore_wait(barrier, NSP - 1)


def project_kernel(h_ref, wq_ref, wk_ref, wv_ref, kc_ref, vc_ref, qkv_ref, ko_ref, vo_ref,
                   wbuf, acc, mine, recv, wsem, csem, ssem, rsem):
    me = lax.axis_index("sp")
    qcol = pl.multiple_of(me * QW, HEAD)
    kcol = pl.multiple_of(me * HEAD, HEAD)
    copies = []
    for i in range(NW):
        rows = pl.ds(i * WC, WC)
        three = [
            pltpu.make_async_copy(wq_ref.at[rows, pl.ds(qcol, QW)], wbuf.at[rows, pl.ds(0, QW)], wsem.at[i, 0]),
            pltpu.make_async_copy(wk_ref.at[rows, pl.ds(kcol, HEAD)], wbuf.at[rows, pl.ds(QW, HEAD)], wsem.at[i, 1]),
            pltpu.make_async_copy(wv_ref.at[rows, pl.ds(kcol, HEAD)], wbuf.at[rows, pl.ds(QW + HEAD, HEAD)], wsem.at[i, 2]),
        ]
        for c in three:
            c.start()
        copies.append(three)
    caches = []
    for j, (src, dst) in enumerate(((kc_ref, ko_ref), (vc_ref, vo_ref))):
        for i in range(2):
            part = pl.ds(i * (ROWS // 2), ROWS // 2)
            c = pltpu.make_async_copy(src.at[part], dst.at[part], csem.at[j, i])
            c.start()
            caches.append(c)
    greet(me)
    for i in range(NW):
        for c in copies[i]:
            c.wait()
        part = jnp.dot(h_ref[:, i * WC:(i + 1) * WC], wbuf[i * WC:(i + 1) * WC, :], preferred_element_type=jnp.float32)
        if i == 0:
            acc[...] = part
        elif i < NW - 1:
            acc[...] += part
        else:
            mine[...] = (acc[...] + part).astype(jnp.bfloat16)
    sends = []
    for d in range(1, NSP):
        c = pltpu.make_async_remote_copy(
            src_ref=mine, dst_ref=recv.at[d - 1], send_sem=ssem.at[d - 1], recv_sem=rsem.at[d - 1],
            device_id={"sp": lax.rem(me + d, NSP)}, device_id_type=MESH)
        c.start()
        sends.append(c)
    qkv_ref[me] = mine[...]
    for d in range(1, NSP):
        sends[d - 1].wait()
        qkv_ref[lax.rem(me + NSP - d, NSP)] = recv[d - 1]
    for c in caches:
        c.wait()


def export_kernel(pos_ref, qkv_ref, k_in, v_in, ko_ref, vo_ref, k_ref, v_ref, new, sem):
    del k_in, v_in
    base = lax.axis_index("sp") * SEQ
    for j in range(2):
        for r in range(16):
            col = QW + j * HEAD
            new[j, pl.ds(r, ROWS, stride=16), :] = qkv_ref[r % KVH, :, col:col + HEAD].astype(jnp.float32)
    row = lax.broadcasted_iota(jnp.int32, (16, HEAD), 0) // KVH

    def one(b, carry):
        t = pos_ref[b] - base
        inside = jnp.logical_and(t >= 0, t < SEQ)
        tc = jnp.clip(t, 0, SEQ - 1)
        rows = pl.ds(pl.multiple_of((tc // 4) * 16, 16), 16)
        sel = row == jnp.where(inside, tc % 4, -1)
        for j, ref in enumerate((k_ref, v_ref)):
            nb = new[j, pl.ds(pl.multiple_of(b * 16, 16), 16), :]
            ref[b, rows, :] = jnp.where(sel, nb, ref[b, rows, :].astype(jnp.float32)).astype(jnp.bfloat16)
        return carry

    copies = []
    for i in range(NE):
        lax.fori_loop(i * ROWS // NE, (i + 1) * ROWS // NE, one, 0, unroll=4)
        part = pl.ds(i * (ROWS // NE), ROWS // NE)
        for j, (src, dst) in enumerate(((k_ref, ko_ref), (v_ref, vo_ref))):
            c = pltpu.make_async_copy(src.at[part], dst.at[part], sem.at[j, i])
            c.start()
            copies.append(c)
    for c in copies:
        c.wait()


def attend_kernel(len_ref, qkv_ref, k_ref, v_ref, wo_ref, out_ref,
                  qs, kn, vn, mn, cidx, acc, ml, racc, rml, osc, attn, wbuf, part, r1, u, r2, fin, r3,
                  wsem, asem, arsem, msem, mrsem, s1, q1, s2, q2, s3, q3):
    me = lax.axis_index("sp")
    core = lax.rem(me, 2)
    mate = me + 1 - 2 * core
    across = lax.rem(me + 2, NSP)
    wcopies = []
    for i in range(2 * NC):
        cols = pl.ds(i * CC, CC)
        c = pltpu.make_async_copy(wo_ref.at[:, cols], wbuf.at[:, cols], wsem.at[i])
        c.start()
        wcopies.append(c)
    greet(me)
    for g in range(KVH):
        for j in range(8):
            if j < GRP:
                qs[pl.ds(g * 8 + j, ROWS, stride=32), :] = qkv_ref[g, :, j * HEAD:(j + 1) * HEAD].astype(jnp.float32)
            else:
                qs[pl.ds(g * 8 + j, ROWS, stride=32), :] = jnp.zeros((ROWS, HEAD), jnp.float32)
    kn[...] = qkv_ref[me, :, QW:QW + HEAD].astype(jnp.float32)
    vn[...] = qkv_ref[me, :, QW + HEAD:PW].astype(jnp.float32)
    mn[...] = jnp.zeros((8, HEAD), jnp.float32)
    col = lax.broadcasted_iota(jnp.int32, (32, FLAT), 1)
    row = lax.broadcasted_iota(jnp.int32, (32, FLAT), 0)
    cidx[...] = jnp.where(lax.rem(col, KVH) == row // 8, col, 1 << 20)
    ml[:, 0] = jnp.zeros((KVH, 8, HEAD), jnp.float32)
    ml[:, 1] = jnp.ones((KVH, 8, HEAD), jnp.float32)
    lane = lax.broadcasted_iota(jnp.int32, (8, HEAD), 1)
    base = me * SEQ
    factor = HEAD ** -0.5 * LOG2E
    lowest = float(jnp.finfo(jnp.float32).min)

    def pair(p, carry):
        q0 = qs[pl.ds(pl.multiple_of(p * 64, 64), 32), :].astype(jnp.bfloat16)
        q1_ = qs[pl.ds(pl.multiple_of(p * 64 + 32, 32), 32), :].astype(jnp.bfloat16)
        z = jnp.zeros((32, HEAD), jnp.bfloat16)
        lhs = jnp.concatenate([jnp.concatenate([q0, z], 1), jnp.concatenate([z, q1_], 1)], 0)
        kk = jnp.concatenate([k_ref[2 * p], k_ref[2 * p + 1]], 1)
        s = lax.dot_general(lhs, kk, (((1,), (1,)), ((), ())), preferred_element_type=jnp.float32)
        ci = cidx[...]
        ws, ms, ls = [], [], []
        for i in range(2):
            lim = (len_ref[2 * p + i] - 1 - base) * KVH
            si = jnp.where(ci < lim, s[32 * i:32 * (i + 1)], -jnp.inf)
            m = jnp.maximum(jnp.max(si, axis=1, keepdims=True), lowest)
            w = jnp.exp2((si - m) * factor)
            ls.append(jnp.sum(w, axis=1, keepdims=True))
            ms.append(m)
            ws.append(w.astype(jnp.bfloat16))
        vv = jnp.concatenate([v_ref[2 * p], v_ref[2 * p + 1]], 1)
        o = jnp.dot(jnp.concatenate(ws, 0), vv, preferred_element_type=jnp.float32)
        for i in range(2):
            b = 2 * p + i
            here = lane == b
            qb = qs[pl.ds(pl.multiple_of(b * 32 + me * 8, 8), 8), :]
            mn[...] = jnp.where(here, jnp.sum(qb * kn[pl.ds(b, 1), :], axis=1, keepdims=True), mn[...])
            oi = o[32 * i:32 * (i + 1), HEAD * i:HEAD * (i + 1)]
            for g in range(KVH):
                acc[g, b] = oi[8 * g:8 * (g + 1)]
                ml[g, 0] = jnp.where(here, ms[i][8 * g:8 * (g + 1)], ml[g, 0])
                ml[g, 1] = jnp.where(here, ls[i][8 * g:8 * (g + 1)], ml[g, 1])
        return carry

    sends = []
    for cb in range(NB):
        lax.fori_loop(cb * BC // 2, (cb + 1) * BC // 2, pair, 0)
        rows = pl.ds(cb * BC, BC)
        for d in range(1, NSP):
            peer = lax.rem(me + d, NSP)
            c = pltpu.make_async_remote_copy(
                src_ref=acc.at[peer, rows], dst_ref=racc.at[d - 1, rows],
                send_sem=asem.at[d - 1, cb], recv_sem=arsem.at[d - 1, cb],
                device_id={"sp": peer}, device_id_type=MESH)
            c.start()
            sends.append(c)
    for d in range(1, NSP):
        peer = lax.rem(me + d, NSP)
        c = pltpu.make_async_remote_copy(
            src_ref=ml.at[peer], dst_ref=rml.at[d - 1], send_sem=msem.at[d - 1], recv_sem=mrsem.at[d - 1],
            device_id={"sp": peer}, device_id_type=MESH)
        c.start()
        sends.append(c)
    for c in sends:
        c.wait()
    mm = [ml[me, 0]] + [rml[d, 0] for d in range(NSP - 1)]
    ll = [ml[me, 1]] + [rml[d, 1] for d in range(NSP - 1)]
    mm.append(mn[...])
    top = jnp.maximum(jnp.maximum(mm[0], mm[1]), jnp.maximum(jnp.maximum(mm[2], mm[3]), mm[4]))
    ww = [jnp.exp2((m - top) * factor) for m in mm]
    total = ww[0] * ll[0] + ww[1] * ll[1] + ww[2] * ll[2] + ww[3] * ll[3] + ww[4]
    inv = 1.0 / total
    scale = [w * inv for w in ww]
    for b in range(ROWS):
        o = acc[me, b] * scale[0][:, b:b + 1]
        for d in range(NSP - 1):
            o = o + racc[d, b] * scale[d + 1][:, b:b + 1]
        o = o + vn[b:b + 1, :] * scale[NSP][:, b:b + 1]
        osc[pl.ds(b * 8, 8), :] = o
    for j in range(GRP):
        attn[:, j * HEAD:(j + 1) * HEAD] = osc[pl.ds(j, ROWS, stride=8), :].astype(jnp.bfloat16)
    a = attn[...]
    for c in wcopies:
        c.wait()
    c1 = []
    for k in range(NC):
        for other in (1, 0):
            half = lax.rem(core + other, 2)
            cols = pl.ds(pl.multiple_of(half * HALF + k * CC, HEAD), CC)
            part[other, k] = jnp.dot(a, wbuf[:, cols], preferred_element_type=jnp.float32)
            if other:
                c = pltpu.make_async_remote_copy(
                    src_ref=part.at[1, k], dst_ref=r1.at[k], send_sem=s1.at[k], recv_sem=q1.at[k],
                    device_id={"sp": mate}, device_id_type=MESH)
                c.start()
                c1.append(c)
    c2 = []
    for k in range(NC):
        c1[k].wait()
        u[k] = part[0, k] + r1[k]
        c = pltpu.make_async_remote_copy(
            src_ref=u.at[k], dst_ref=r2.at[k], send_sem=s2.at[k], recv_sem=q2.at[k],
            device_id={"sp": across}, device_id_type=MESH)
        c.start()
        c2.append(c)
    c3 = []
    for k in range(NC):
        c2[k].wait()
        fin[k] = (u[k] + r2[k]).astype(jnp.bfloat16)
        c = pltpu.make_async_remote_copy(
            src_ref=fin.at[k], dst_ref=r3.at[k], send_sem=s3.at[k], recv_sem=q3.at[k],
            device_id={"sp": mate}, device_id_type=MESH)
        c.start()
        c3.append(c)
        out_ref[:, pl.ds(pl.multiple_of(core * HALF + k * CC, HEAD), CC)] = fin[k]
    for k in range(NC):
        c3[k].wait()
        out_ref[:, pl.ds(pl.multiple_of((1 - core) * HALF + k * CC, HEAD), CC)] = r3[k]


def solution(mesh):
    row_spec = P(('rep', 'dp'), None)
    cache_spec = P(('rep', 'dp'), 'sp', None, None)
    len_spec = P(('rep', 'dp'))
    hbm = pl.BlockSpec(memory_space=pl.ANY)
    vmem = pl.BlockSpec(memory_space=pltpu.VMEM)
    smem = pl.BlockSpec(memory_space=pltpu.SMEM)
    bf16, f32 = jnp.bfloat16, jnp.float32
    dma = pltpu.SemaphoreType.DMA

    def local_step(hidden, w_query, w_key, w_value, w_out, k_cache, v_cache, write_pos, valid_len):
        kc = k_cache.reshape(ROWS, FLAT, HEAD)
        vc = v_cache.reshape(ROWS, FLAT, HEAD)
        pin = lambda x: pltpu.with_memory_space_constraint(x, pltpu.HBM)
        flat = jax.ShapeDtypeStruct((ROWS, FLAT, HEAD), bf16)
        qkv, kv, vv = pl.pallas_call(
            project_kernel,
            out_shape=[jax.ShapeDtypeStruct((NSP, ROWS, PW), bf16), flat, flat],
            in_specs=[vmem, hbm, hbm, hbm, hbm, hbm],
            out_specs=[vmem, vmem, vmem],
            scratch_shapes=[
                pltpu.VMEM((DIM, PW), bf16), pltpu.VMEM((ROWS, PW), f32), pltpu.VMEM((ROWS, PW), bf16),
                pltpu.VMEM((NSP - 1, ROWS, PW), bf16),
                dma((NW, 3)), dma((2, 2)), dma((NSP - 1,)), dma((NSP - 1,))],
            compiler_params=pltpu.CompilerParams(collective_id=0, has_side_effects=True, vmem_limit_bytes=14 << 20),
            name="project",
            cost_estimate=pl.CostEstimate(flops=10_000_000_000, bytes_accessed=34_000_000, transcendentals=0),
        )(hidden, pin(w_query), pin(w_key), pin(w_value), pin(kc), pin(vc))
        attn_out = pl.pallas_call(
            attend_kernel,
            out_shape=jax.ShapeDtypeStruct((ROWS, DIM), bf16),
            in_specs=[smem, vmem, vmem, vmem, hbm],
            out_specs=vmem,
            scratch_shapes=[
                pltpu.VMEM((ROWS * 32, HEAD), f32), pltpu.VMEM((ROWS, HEAD), f32), pltpu.VMEM((ROWS, HEAD), f32),
                pltpu.VMEM((8, HEAD), f32), pltpu.VMEM((32, FLAT), jnp.int32),
                pltpu.VMEM((KVH, ROWS, 8, HEAD), f32), pltpu.VMEM((KVH, 2, 8, HEAD), f32),
                pltpu.VMEM((NSP - 1, ROWS, 8, HEAD), f32), pltpu.VMEM((NSP - 1, 2, 8, HEAD), f32),
                pltpu.VMEM((ROWS * 8, HEAD), f32), pltpu.VMEM((ROWS, QW), bf16),
                pltpu.VMEM((QW, DIM), bf16),
                pltpu.VMEM((2, NC, ROWS, CC), f32), pltpu.VMEM((NC, ROWS, CC), f32),
                pltpu.VMEM((NC, ROWS, CC), f32), pltpu.VMEM((NC, ROWS, CC), f32),
                pltpu.VMEM((NC, ROWS, CC), bf16), pltpu.VMEM((NC, ROWS, CC), bf16),
                dma((2 * NC,)), dma((NSP - 1, NB)), dma((NSP - 1, NB)), dma((NSP - 1,)), dma((NSP - 1,)),
                dma((NC,)), dma((NC,)), dma((NC,)), dma((NC,)), dma((NC,)), dma((NC,))],
            compiler_params=pltpu.CompilerParams(collective_id=1, has_side_effects=True, vmem_limit_bytes=16 << 20),
            name="attend",
            cost_estimate=pl.CostEstimate(flops=20_000_000_000, bytes_accessed=40_000_000, transcendentals=0),
        )(valid_len, qkv, kv, vv, pin(w_out))
        k_new, v_new, _, _ = pl.pallas_call(
            export_kernel,
            out_shape=[flat, flat, flat, flat],
            in_specs=[smem, vmem, vmem, vmem],
            out_specs=[hbm, hbm, vmem, vmem],
            scratch_shapes=[pltpu.VMEM((2, ROWS * 16, HEAD), f32), dma((2, NE))],
            input_output_aliases={2: 2, 3: 3},
            compiler_params=pltpu.CompilerParams(vmem_limit_bytes=2 << 20),
            name="export",
            cost_estimate=pl.CostEstimate(flops=1_000_000_000, bytes_accessed=34_000_000, transcendentals=0),
        )(write_pos, qkv, kv, vv)
        shape = (ROWS, SEQ, KVH, HEAD)
        return attn_out, k_new.reshape(shape), v_new.reshape(shape)

    return jax.shard_map(local_step, mesh=mesh, in_specs=(row_spec, P(), P(), P(), P('sp', None), cache_spec, cache_spec, len_spec, len_spec), out_specs=(row_spec, cache_spec, cache_spec), check_vma=False)
```

time: 132 us -> 49.1 us (0.37)
  Pallas kernels: 0 us -> 46.6 us
  waiting for transfers between devices: 36.8 us -> 0 us
  blocking collectives: 29.2 us -> 0 us
  matrix products: 27.3 us -> 0 us
  other arithmetic: 16.8 us -> 0 us
  between operations: 14.2 us -> 0.69 us
  local copies, waits for them, and re-layouts: 7.75 us -> 1.63 us
    pallas_call x0 -> x3, Pallas kernels: none -> 46.6 us  [the longest x1 26 us: local_step(): pl.pallas_call(attend_kernel, out_shape=jax.ShapeDtypeStruct((ROWS, DIM),...]
    psum x1 -> x0, waiting for transfers between devices: 36.8 us -> none  [local_step(): packed = lax.psum(packed, 'sp')]
    dot_general x6 -> x0, matrix products: 27.3 us -> none  [the longest x1 10.6 us: local_step(): jnp.dot(hidden, w_query, preferred_element_type=jnp.float32)]
    psum x1 -> x0, blocking collectives: 15.7 us -> none  [local_step(): attn_out = lax.psum(partial_out, 'sp').astype(jnp.bfloat16)]
    select_n x1 -> x0, other arithmetic: 13.7 us -> none  [local_step(): jnp.where(at_pos, value_new.reshape(num_rows, 1, kv_heads, head_dim), v_c...]
    pmax x1 -> x0, blocking collectives: 13.5 us -> none  [local_step(): global_max = lax.pmax(local_max, 'sp')]
    unnamed x10 -> x7, local copies, waits for them, and re-layouts: 4.29 us -> 1.63 us
  transfers between devices with their start and end apart: 1 -> 0, of which waited for: 1 -> 0; matrix products, arithmetic and copies ran while one was open for 0% -> 0% of each run, Pallas kernels for 0% -> 0%
where the time goes in v1:
time: 49.1 us; the launch traced here: 48.9 us
  Pallas kernels  46.6 us (95%)
  local copies, waits for them, and re-layouts  1.63 us (3%)
  between operations  0.69 us (1%)
    pallas_call x1, Pallas kernels, local_step(): pl.pallas_call(attend_kernel, out_shape=jax.ShapeDtypeStruct((ROWS, DIM),...  26 us
    pallas_call x1, Pallas kernels, local_step(): pl.pallas_call(project_kernel, out_shape=[jax.ShapeDtypeStruct((NSP, ROWS...  13.9 us
    pallas_call x1, Pallas kernels, local_step(): pl.pallas_call(export_kernel, out_shape=[flat, flat, flat, flat], in_spec...  6.71 us
    unnamed x7, local copies, waits for them, and re-layouts  1.63 us

profile of v1, /device:TPU:0, one launch (start us, length us, event | category | flops | bytes accessed | tf_op | source)
XLA Modules:
  0.0 48.9 jit_solution(2601181468090019312)
XLA Ops:
  0.6 0.0 copy-start
  0.6 0.9 %copy-done = bf16[32,3584]{1,0:T(8,128)(2,1)S(1)} copy-done((bf16[32,3584]{1,0:T(8,128)(2,1)S(1)}, bf16[32,3584]{1,0:T(8,128)(2,1)}, u32[]{:S(2)}) %copy-start) | copy-done | bytes 229400
  1.6 0.0 copy-start.2
  1.6 13.9 %project.1 = (bf16[4,32,1152]{2,1,0:T(8,128)(2,1)S(1)}, bf16[32,1024,128]{2,1,0:T(8,128)(2,1)S(1)}, bf16[32,1024,128]{2,1,0:T(8,128)(2,1)S(1)}) custom-call(bf16[32,3584]{1,0:T(8,128)(2,1)S(1)} %copy-done, bf16[3584,3584]{1,0:T(8,128)(2,1)} %wq_ref.1, bf16[3584,512]{1,0:T(8,128)(2,1)} %wk_ref.1, bf16[3584,512]{1,0:T(8,128)(2,1)} %wv_ref.1, ...), custom_call_target="tpu_custom_call" | custom-call | flops 10000000000 | bytes 34000000 | tf_op jit(solution)/shard_map/project/pallas_call | solution.py:273
  15.5 0.0 copy-done.2
  15.5 0.0 copy-start.1
  15.5 26.0 %attend.1 = bf16[32,3584]{1,0:T(8,128)(2,1)S(1)} custom-call(s32[32]{0:T(128)S(1)} %copy-done.2, bf16[4,32,1152]{2,1,0:T(8,128)(2,1)S(1)} %get-tuple-element.8.qkv_ref, bf16[32,1024,128]{2,1,0:T(8,128)(2,1)S(1)} %get-tuple-element.9.k_ref.k_in, bf16[32,1024,128]{2,1,0:T(8,128)(2,1)S(1)} %get-tuple-element.10.v_ref.v_in, bf16[896,3584]{1,0:T(8,128)(2,1)} %wo_ref.1), custom_call_target="tpu_custom_call" | custom-call | flops 20000000000 | bytes 40000000 | tf_op jit(solution)/shard_map/attend/pallas_call | solution.py:286
  41.5 0.0 copy-done.1
  41.5 6.7 %export.1 = (bf16[32,1024,128]{2,1,0:T(8,128)(2,1)}, bf16[32,1024,128]{2,1,0:T(8,128)(2,1)}, bf16[32,1024,128]{2,1,0:T(8,128)(2,1)S(1)}, bf16[32,1024,128]{2,1,0:T(8,128)(2,1)S(1)}) custom-call(s32[32]{0:T(128)S(1)} %copy-done.1, bf16[4,32,1152]{2,1,0:T(8,128)(2,1)S(1)} %get-tuple-element.8.qkv_ref, ...), custom_call_target="tpu_custom_call", output_to_operand_aliasing={{2}: (2, {}), {3}: (3, {})} | custom-call | flops 1000000000 | bytes 34000000 | tf_op jit(solution)/shard_map/export/pallas_call | solution.py:307
  48.2 0.7 %copy.17 = bf16[32,3584]{1,0:T(8,128)(2,1)} copy(bf16[32,3584]{1,0:T(8,128)(2,1)S(1)} %attend.1) | data formatting | bytes 458752
Async XLA Ops:
  0.6 0.9 %copy-start = (bf16[32,3584]{1,0:T(8,128)(2,1)S(1)}, bf16[32,3584]{1,0:T(8,128)(2,1)}, u32[]{:S(2)}) copy-start(bf16[32,3584]{1,0:T(8,128)(2,1)} %h_ref.1) | copy-start | bytes 688132
  1.6 13.9 %copy-start.2 = (s32[32]{0:T(128)S(1)}, s32[32]{0:T(128)}, u32[]{:S(2)}) copy-start(s32[32]{0:T(128)} %len_ref.1) | copy-start | bytes 388
  15.5 26.0 %copy-start.1 = (s32[32]{0:T(128)S(1)}, s32[32]{0:T(128)}, u32[]{:S(2)}) copy-start(s32[32]{0:T(128)} %pos_ref.1) | copy-start | bytes 388

commit v2 on v1

v2 whole, which is shorter than its diff:
```python
import jax
import jax.numpy as jnp
from jax import lax
from jax.experimental import pallas as pl
from jax.experimental.pallas import tpu as pltpu
from jax.sharding import PartitionSpec as P

MESH = pl.DeviceIdType.MESH
LOG2E = 1.4426950408889634
NSP = 4
ROWS = 32
DIM = 3584
HEAD = 128
KVH = 4
GRP = 7
SEQ = 256
FLAT = SEQ * KVH
QW = GRP * HEAD
PW = QW + 2 * HEAD
NW = 7
WC = DIM // NW
NE = 4
NH = 2
HR = ROWS // NH
HALF = DIM // 2
NC = 1
CC = HALF // NC
FACTOR = HEAD ** -0.5 * LOG2E


def greet(me):
    barrier = pltpu.get_barrier_semaphore()
    for d in range(1, NSP):
        pl.semaphore_signal(barrier, inc=1, device_id={"sp": lax.rem(me + d, NSP)}, device_id_type=MESH)
    pl.semaphore_wait(barrier, NSP - 1)


def project_kernel(h_ref, wq_ref, wk_ref, wv_ref, kc_ref, vc_ref, qkv_ref, ko_ref, vo_ref,
                   wbuf, acc, mine, recv, wsem, csem, ssem, rsem):
    me = lax.axis_index("sp")
    qcol = pl.multiple_of(me * QW, HEAD)
    kcol = pl.multiple_of(me * HEAD, HEAD)
    copies = []
    for i in range(NW):
        rows = pl.ds(i * WC, WC)
        three = [
            pltpu.make_async_copy(wq_ref.at[rows, pl.ds(qcol, QW)], wbuf.at[rows, pl.ds(0, QW)], wsem.at[i, 0]),
            pltpu.make_async_copy(wk_ref.at[rows, pl.ds(kcol, HEAD)], wbuf.at[rows, pl.ds(QW, HEAD)], wsem.at[i, 1]),
            pltpu.make_async_copy(wv_ref.at[rows, pl.ds(kcol, HEAD)], wbuf.at[rows, pl.ds(QW + HEAD, HEAD)], wsem.at[i, 2]),
        ]
        for c in three:
            c.start()
        copies.append(three)
    caches = []
    for j, (src, dst) in enumerate(((kc_ref, ko_ref), (vc_ref, vo_ref))):
        for i in range(2):
            part = pl.ds(i * (ROWS // 2), ROWS // 2)
            c = pltpu.make_async_copy(src.at[part], dst.at[part], csem.at[j, i])
            c.start(priority=1)
            caches.append(c)
    greet(me)
    for i in range(NW):
        for c in copies[i]:
            c.wait()
        part = jnp.dot(h_ref[:, i * WC:(i + 1) * WC], wbuf[i * WC:(i + 1) * WC, :], preferred_element_type=jnp.float32)
        if i == 0:
            acc[...] = part
        elif i < NW - 1:
            acc[...] += part
        else:
            mine[...] = (acc[...] + part).astype(jnp.bfloat16)
    sends = []
    for d in range(1, NSP):
        c = pltpu.make_async_remote_copy(
            src_ref=mine, dst_ref=recv.at[d - 1], send_sem=ssem.at[d - 1], recv_sem=rsem.at[d - 1],
            device_id={"sp": lax.rem(me + d, NSP)}, device_id_type=MESH)
        c.start()
        sends.append(c)
    qkv_ref[me] = mine[...]
    for d in range(1, NSP):
        sends[d - 1].wait()
        qkv_ref[lax.rem(me + NSP - d, NSP)] = recv[d - 1]
    for c in caches:
        c.wait()


def attend_kernel(pos_ref, len_ref, qkv_ref, k_in, v_in, ko_ref, vo_ref, k_ref, v_ref, acc, ml, new, qs, cidx, sem):
    del k_in, v_in
    base = lax.axis_index("sp") * SEQ
    for j in range(2):
        for r in range(16):
            col = QW + j * HEAD
            new[j, pl.ds(r, ROWS, stride=16), :] = qkv_ref[r % KVH, :, col:col + HEAD].astype(jnp.float32)
    row = lax.broadcasted_iota(jnp.int32, (16, HEAD), 0) // KVH

    def patch(b, carry):
        t = pos_ref[b] - base
        inside = jnp.logical_and(t >= 0, t < SEQ)
        tc = jnp.clip(t, 0, SEQ - 1)
        rows = pl.ds(pl.multiple_of((tc // 4) * 16, 16), 16)
        sel = row == jnp.where(inside, tc % 4, -1)
        for j, ref in enumerate((k_ref, v_ref)):
            nb = new[j, pl.ds(pl.multiple_of(b * 16, 16), 16), :]
            ref[b, rows, :] = jnp.where(sel, nb, ref[b, rows, :].astype(jnp.float32)).astype(jnp.bfloat16)
        return carry

    copies = []
    for i in range(NE):
        lax.fori_loop(i * ROWS // NE, (i + 1) * ROWS // NE, patch, 0, unroll=4)
        part = pl.ds(i * (ROWS // NE), ROWS // NE)
        for j, (src, dst) in enumerate(((k_ref, ko_ref), (v_ref, vo_ref))):
            c = pltpu.make_async_copy(src.at[part], dst.at[part], sem.at[j, i])
            c.start()
            copies.append(c)
    for g in range(KVH):
        for j in range(8):
            if j < GRP:
                qs[pl.ds(g * 8 + j, ROWS, stride=32), :] = qkv_ref[g, :, j * HEAD:(j + 1) * HEAD].astype(jnp.float32)
            else:
                qs[pl.ds(g * 8 + j, ROWS, stride=32), :] = jnp.zeros((ROWS, HEAD), jnp.float32)
    col = lax.broadcasted_iota(jnp.int32, (32, FLAT), 1)
    head = lax.broadcasted_iota(jnp.int32, (32, FLAT), 0) // 8
    cidx[...] = jnp.where(lax.rem(col, KVH) == head, col, 1 << 20)
    ml[:, 0] = jnp.zeros((KVH, 8, HEAD), jnp.float32)
    ml[:, 1] = jnp.ones((KVH, 8, HEAD), jnp.float32)
    lane = lax.broadcasted_iota(jnp.int32, (8, HEAD), 1)
    lowest = float(jnp.finfo(jnp.float32).min)

    def pair(p, carry):
        q0 = qs[pl.ds(pl.multiple_of(p * 64, 64), 32), :].astype(jnp.bfloat16)
        q1 = qs[pl.ds(pl.multiple_of(p * 64 + 32, 32), 32), :].astype(jnp.bfloat16)
        z = jnp.zeros((32, HEAD), jnp.bfloat16)
        lhs = jnp.concatenate([jnp.concatenate([q0, z], 1), jnp.concatenate([z, q1], 1)], 0)
        kk = jnp.concatenate([k_ref[2 * p], k_ref[2 * p + 1]], 1)
        s = lax.dot_general(lhs, kk, (((1,), (1,)), ((), ())), preferred_element_type=jnp.float32)
        ci = cidx[...]
        ws, ms, ls = [], [], []
        for i in range(2):
            lim = (len_ref[2 * p + i] - base) * KVH
            si = jnp.where(ci < lim, s[32 * i:32 * (i + 1)], -jnp.inf)
            m = jnp.maximum(jnp.max(si, axis=1, keepdims=True), lowest)
            w = jnp.exp2((si - m) * FACTOR)
            ls.append(jnp.sum(w, axis=1, keepdims=True))
            ms.append(m)
            ws.append(w.astype(jnp.bfloat16))
        vv = jnp.concatenate([v_ref[2 * p], v_ref[2 * p + 1]], 1)
        o = jnp.dot(jnp.concatenate(ws, 0), vv, preferred_element_type=jnp.float32)
        for i in range(2):
            b = 2 * p + i
            here = lane == b
            oi = o[32 * i:32 * (i + 1), HEAD * i:HEAD * (i + 1)]
            for g in range(KVH):
                acc[g, b] = oi[8 * g:8 * (g + 1)]
                ml[g, 0] = jnp.where(here, ms[i][8 * g:8 * (g + 1)], ml[g, 0])
                ml[g, 1] = jnp.where(here, ls[i][8 * g:8 * (g + 1)], ml[g, 1])
        return carry

    lax.fori_loop(0, ROWS // 2, pair, 0, unroll=16)
    for c in copies:
        c.wait()


def combine(parts):
    top = parts[0][0]
    for m, _ in parts[1:]:
        top = jnp.maximum(top, m)
    ww = [jnp.exp2((m - top) * FACTOR) for m, _ in parts]
    total = ww[0] * parts[0][1]
    for w, (_, l) in zip(ww[1:], parts[1:]):
        total = total + w * l
    return top, total, ww


def reduce_kernel(acc, ml, wo_ref, out_ref,
                  ra, rma, cross, mcross, rb, rmb, osc, attn, wbuf, part, r1, u, r2, fin, r3,
                  wsem, sa, qa, sma, qma, sb, qb, smb, qmb, s1, q1, s2, q2, s3, q3):
    me = lax.axis_index("sp")
    core = lax.rem(me, 2)
    mate = me + 1 - 2 * core
    across = lax.rem(me + 2, NSP)
    wcopies = []
    for i in range(4):
        rows = pl.ds(i * (QW // 4), QW // 4)
        c = pltpu.make_async_copy(wo_ref.at[rows], wbuf.at[rows], wsem.at[i])
        c.start(priority=1)
        wcopies.append(c)
    greet(me)

    def send(src, dst, ssem, rsem, peer):
        c = pltpu.make_async_remote_copy(src_ref=src, dst_ref=dst, send_sem=ssem, recv_sem=rsem,
                                         device_id={"sp": peer}, device_id_type=MESH)
        c.start()
        return c

    theirs = (lax.rem(mate + 2, NSP), mate)
    ours = (across, me)
    am = [send(ml.at[theirs[j]], rma.at[j], sma.at[j], qma.at[j], mate) for j in range(2)]
    aa = [[send(acc.at[theirs[j], pl.ds(h * HR, HR)], ra.at[j, pl.ds(h * HR, HR)], sa.at[j, h], qa.at[j, h], mate)
           for h in range(NH)] for j in range(2)]
    am[0].wait()
    top, total, ww = combine([(ml[across, 0], ml[across, 1]), (rma[0, 0], rma[0, 1])])
    mcross[0] = top
    mcross[1] = total
    bm = send(mcross, rmb, smb, qmb, across)
    bb = []
    for h in range(NH):
        aa[0][h].wait()
        for b in range(h * HR, (h + 1) * HR):
            cross[b] = acc[across, b] * ww[0][:, b:b + 1] + ra[0, b] * ww[1][:, b:b + 1]
        rows = pl.ds(h * HR, HR)
        bb.append(send(cross.at[rows], rb.at[rows], sb.at[h], qb.at[h], across))
    am[1].wait()
    bm.wait()
    _, total, ww = combine([(ml[me, 0], ml[me, 1]), (rma[1, 0], rma[1, 1]), (rmb[0], rmb[1])])
    inv = 1.0 / total
    scale = [w * inv for w in ww]
    for h in range(NH):
        aa[1][h].wait()
        for b in range(h * HR, (h + 1) * HR):
            osc[pl.ds(b * 8, 8), :] = acc[me, b] * scale[0][:, b:b + 1] + ra[1, b] * scale[1][:, b:b + 1]
    c1, c2, c3 = {}, {}, {}
    for h in range(NH):
        bb[h].wait()
        for b in range(h * HR, (h + 1) * HR):
            osc[pl.ds(b * 8, 8), :] += rb[b] * scale[2][:, b:b + 1]
        for j in range(GRP):
            attn[h, :, j * HEAD:(j + 1) * HEAD] = osc[pl.ds(h * HR * 8 + j, HR, stride=8), :].astype(jnp.bfloat16)
        a = attn[h]
        if h == 0:
            for c in wcopies:
                c.wait()
        for k in range(NC):
            for other in (1, 0):
                half = lax.rem(core + other, 2)
                cols = pl.ds(pl.multiple_of(half * HALF + k * CC, HEAD), CC)
                part[other, h, k] = jnp.dot(a, wbuf[:, cols], preferred_element_type=jnp.float32)
                if other:
                    c1[h, k] = send(part.at[1, h, k], r1.at[h, k], s1.at[h, k], q1.at[h, k], mate)
        for k in range(NC):
            c1[h, k].wait()
            u[h, k] = part[0, h, k] + r1[h, k]
            c2[h, k] = send(u.at[h, k], r2.at[h, k], s2.at[h, k], q2.at[h, k], across)
    for h in range(NH):
        for k in range(NC):
            c2[h, k].wait()
            fin[h, k] = (u[h, k] + r2[h, k]).astype(jnp.bfloat16)
            c3[h, k] = send(fin.at[h, k], r3.at[h, k], s3.at[h, k], q3.at[h, k], mate)
            out_ref[pl.ds(h * HR, HR), pl.ds(pl.multiple_of(core * HALF + k * CC, HEAD), CC)] = fin[h, k]
    for h in range(NH):
        for k in range(NC):
            c3[h, k].wait()
            out_ref[pl.ds(h * HR, HR), pl.ds(pl.multiple_of((1 - core) * HALF + k * CC, HEAD), CC)] = r3[h, k]


def solution(mesh):
    row_spec = P(('rep', 'dp'), None)
    cache_spec = P(('rep', 'dp'), 'sp', None, None)
    len_spec = P(('rep', 'dp'))
    hbm = pl.BlockSpec(memory_space=pl.ANY)
    vmem = pl.BlockSpec(memory_space=pltpu.VMEM)
    smem = pl.BlockSpec(memory_space=pltpu.SMEM)
    bf16, f32 = jnp.bfloat16, jnp.float32
    dma = pltpu.SemaphoreType.DMA

    def local_step(hidden, w_query, w_key, w_value, w_out, k_cache, v_cache, write_pos, valid_len):
        kc = k_cache.reshape(ROWS, FLAT, HEAD)
        vc = v_cache.reshape(ROWS, FLAT, HEAD)
        pin = lambda x: pltpu.with_memory_space_constraint(x, pltpu.HBM)
        flat = jax.ShapeDtypeStruct((ROWS, FLAT, HEAD), bf16)
        qkv, kv, vv = pl.pallas_call(
            project_kernel,
            out_shape=[jax.ShapeDtypeStruct((NSP, ROWS, PW), bf16), flat, flat],
            in_specs=[vmem, hbm, hbm, hbm, hbm, hbm],
            out_specs=[vmem, vmem, vmem],
            scratch_shapes=[
                pltpu.VMEM((DIM, PW), bf16), pltpu.VMEM((ROWS, PW), f32), pltpu.VMEM((ROWS, PW), bf16),
                pltpu.VMEM((NSP - 1, ROWS, PW), bf16),
                dma((NW, 3)), dma((2, 2)), dma((NSP - 1,)), dma((NSP - 1,))],
            compiler_params=pltpu.CompilerParams(collective_id=0, has_side_effects=True, vmem_limit_bytes=14 << 20),
            name="project",
            cost_estimate=pl.CostEstimate(flops=10_000_000_000, bytes_accessed=34_000_000, transcendentals=0),
        )(hidden, pin(w_query), pin(w_key), pin(w_value), pin(kc), pin(vc))
        tiles = (KVH, ROWS, 8, HEAD)
        k_new, v_new, _, _, acc, ml = pl.pallas_call(
            attend_kernel,
            out_shape=[flat, flat, flat, flat, jax.ShapeDtypeStruct(tiles, f32), jax.ShapeDtypeStruct((KVH, 2, 8, HEAD), f32)],
            in_specs=[smem, smem, vmem, vmem, vmem],
            out_specs=[hbm, hbm, vmem, vmem, vmem, vmem],
            scratch_shapes=[
                pltpu.VMEM((2, ROWS * 16, HEAD), f32), pltpu.VMEM((ROWS * 32, HEAD), f32),
                pltpu.VMEM((32, FLAT), jnp.int32), dma((2, NE))],
            input_output_aliases={3: 2, 4: 3},
            compiler_params=pltpu.CompilerParams(vmem_limit_bytes=6 << 20),
            name="attend",
            cost_estimate=pl.CostEstimate(flops=7_000_000_000, bytes_accessed=34_000_000, transcendentals=0),
        )(write_pos, valid_len, qkv, kv, vv)
        parts = (NH, NC, HR, CC)
        attn_out = pl.pallas_call(
            reduce_kernel,
            out_shape=jax.ShapeDtypeStruct((ROWS, DIM), bf16),
            in_specs=[vmem, vmem, hbm],
            out_specs=vmem,
            scratch_shapes=[
                pltpu.VMEM((2,) + tiles[1:], f32), pltpu.VMEM((2, 2, 8, HEAD), f32),
                pltpu.VMEM(tiles[1:], f32), pltpu.VMEM((2, 8, HEAD), f32),
                pltpu.VMEM(tiles[1:], f32), pltpu.VMEM((2, 8, HEAD), f32),
                pltpu.VMEM((ROWS * 8, HEAD), f32), pltpu.VMEM((NH, HR, QW), bf16), pltpu.VMEM((QW, DIM), bf16),
                pltpu.VMEM((2,) + parts, f32), pltpu.VMEM(parts, f32), pltpu.VMEM(parts, f32), pltpu.VMEM(parts, f32),
                pltpu.VMEM(parts, bf16), pltpu.VMEM(parts, bf16),
                dma((4,)), dma((2, NH)), dma((2, NH)), dma((2,)), dma((2,)), dma((NH,)), dma((NH,)), dma, dma]
                + [dma((NH, NC))] * 6,
            compiler_params=pltpu.CompilerParams(collective_id=1, has_side_effects=True, vmem_limit_bytes=14 << 20),
            name="reduce",
            cost_estimate=pl.CostEstimate(flops=20_000_000_000, bytes_accessed=10_000_000, transcendentals=0),
        )(acc, ml, pin(w_out))
        shape = (ROWS, SEQ, KVH, HEAD)
        return attn_out, k_new.reshape(shape), v_new.reshape(shape)

    return jax.shard_map(local_step, mesh=mesh, in_specs=(row_spec, P(), P(), P(), P('sp', None), cache_spec, cache_spec, len_spec, len_spec), out_specs=(row_spec, cache_spec, cache_spec), check_vma=False)
```

time: 49.1 us -> 38.5 us (0.78)
  Pallas kernels: 46.6 us -> 36 us
    pallas_call x2, Pallas kernels: 32.7 us -> 25.9 us  [the longest x1 16.7 us: local_step(): pl.pallas_call(reduce_kernel, out_shape=jax.ShapeDtypeStruct((ROWS, DIM),...]
    pallas_call x1, Pallas kernels: 13.9 us -> 10.1 us  [local_step(): pl.pallas_call(project_kernel, out_shape=[jax.ShapeDtypeStruct((NSP, ROWS...]
where the time goes in v2:
time: 38.5 us; the launch traced here: 38.3 us
  Pallas kernels  36 us (94%)
  local copies, waits for them, and re-layouts  1.63 us (4%)
  between operations  0.68 us (2%)
    pallas_call x1, Pallas kernels, local_step(): pl.pallas_call(reduce_kernel, out_shape=jax.ShapeDtypeStruct((ROWS, DIM),...  16.7 us
    pallas_call x1, Pallas kernels, local_step(): pl.pallas_call(project_kernel, out_shape=[jax.ShapeDtypeStruct((NSP, ROWS...  10.1 us
    pallas_call x1, Pallas kernels, local_step(): pl.pallas_call(attend_kernel, out_shape=[flat, flat, flat, flat, jax.Shap...  9.26 us
    unnamed x7, local copies, waits for them, and re-layouts  1.63 us

profile of v2, /device:TPU:0, one launch (start us, length us, event | category | flops | bytes accessed | tf_op | source)
XLA Modules:
  0.0 38.3 jit_solution(15337942530581633508)
XLA Ops:
  0.6 0.0 copy-start
  0.6 0.9 %copy-done = bf16[32,3584]{1,0:T(8,128)(2,1)S(1)} copy-done((bf16[32,3584]{1,0:T(8,128)(2,1)S(1)}, bf16[32,3584]{1,0:T(8,128)(2,1)}, u32[]{:S(2)}) %copy-start) | copy-done | bytes 229400
  1.6 0.0 copy-start.1
  1.6 0.0 copy-start.2
  1.6 10.1 %project.1 = (bf16[4,32,1152]{2,1,0:T(8,128)(2,1)S(1)}, bf16[32,1024,128]{2,1,0:T(8,128)(2,1)S(1)}, bf16[32,1024,128]{2,1,0:T(8,128)(2,1)S(1)}) custom-call(bf16[32,3584]{1,0:T(8,128)(2,1)S(1)} %copy-done, bf16[3584,3584]{1,0:T(8,128)(2,1)} %wq_ref.1, bf16[3584,512]{1,0:T(8,128)(2,1)} %wk_ref.1, bf16[3584,512]{1,0:T(8,128)(2,1)} %wv_ref.1, ...), custom_call_target="tpu_custom_call" | custom-call | flops 10000000000 | bytes 34000000 | tf_op jit(solution)/shard_map/project/pallas_call | solution.py:270
  11.7 0.0 copy-done.1
  11.7 0.0 copy-done.2
  11.7 9.3 %attend.1 = (bf16[32,1024,128]{2,1,0:T(8,128)(2,1)}, bf16[32,1024,128]{2,1,0:T(8,128)(2,1)}, bf16[32,1024,128]{2,1,0:T(8,128)(2,1)S(1)}, bf16[32,1024,128]{2,1,0...) custom-call(s32[32]{0:T(128)S(1)} %copy-done.1, ...), custom_call_target="tpu_custom_call", output_to_operand_aliasing={{2}: (3, {}), {3}: (4, {})} | custom-call | flops 7000000000 | bytes 34000000 | tf_op jit(solution)/shard_map/attend/pallas_call | solution.py:284
  21.0 16.7 %reduce.1 = bf16[32,3584]{1,0:T(8,128)(2,1)S(1)} custom-call(f32[4,32,8,128]{3,2,1,0:T(8,128)S(1)} %get-tuple-element.13.acc, f32[4,2,8,128]{3,2,1,0:T(8,128)S(1)} %get-tuple-element.14.ml, bf16[896,3584]{1,0:T(8,128)(2,1)} %wo_ref.1), custom_call_target="tpu_custom_call" | custom-call | flops 20000000000 | bytes 10000000 | tf_op jit(solution)/shard_map/reduce/pallas_call | solution.py:298
  37.7 0.7 %copy.17 = bf16[32,3584]{1,0:T(8,128)(2,1)} copy(bf16[32,3584]{1,0:T(8,128)(2,1)S(1)} %reduce.1) | data formatting | bytes 458752
Async XLA Ops:
  0.6 0.9 %copy-start = (bf16[32,3584]{1,0:T(8,128)(2,1)S(1)}, bf16[32,3584]{1,0:T(8,128)(2,1)}, u32[]{:S(2)}) copy-start(bf16[32,3584]{1,0:T(8,128)(2,1)} %h_ref.1) | copy-start | bytes 688132
  1.6 10.1 %copy-start.1 = (s32[32]{0:T(128)S(1)}, s32[32]{0:T(128)}, u32[]{:S(2)}) copy-start(s32[32]{0:T(128)} %pos_ref.1) | copy-start | bytes 388
  1.6 10.1 %copy-start.2 = (s32[32]{0:T(128)S(1)}, s32[32]{0:T(128)}, u32[]{:S(2)}) copy-start(s32[32]{0:T(128)} %len_ref.1) | copy-start | bytes 388

commit v3 on v2

v3 whole, which is shorter than its diff:
```python
import jax
import jax.numpy as jnp
from jax import lax
from jax.experimental import pallas as pl
from jax.experimental.pallas import tpu as pltpu
from jax.sharding import PartitionSpec as P

MESH = pl.DeviceIdType.MESH
LOG2E = 1.4426950408889634
NSP = 4
ROWS = 32
DIM = 3584
HEAD = 128
KVH = 4
GRP = 7
SEQ = 256
FLAT = SEQ * KVH
QW = GRP * HEAD
PW = QW + 2 * HEAD
PIECES = ((0, 256), (256, 512), (512, 768), (768, QW), (QW, PW))
NP = len(PIECES)
NE = 4
EARLY = 24
LATE = ROWS - EARLY
NH = 2
HR = ROWS // NH
HALF = DIM // 2
NC = 2
CC = HALF // NC
FACTOR = HEAD ** -0.5 * LOG2E
CHUNKS = ((0, HR), (HR, EARLY), (EARLY, ROWS))


def greet(me):
    barrier = pltpu.get_barrier_semaphore()
    for d in range(1, NSP):
        pl.semaphore_signal(barrier, inc=1, device_id={"sp": lax.rem(me + d, NSP)}, device_id_type=MESH)


def greeted():
    pl.semaphore_wait(pltpu.get_barrier_semaphore(), NSP - 1)


def send(src, dst, ssem, rsem, peer):
    c = pltpu.make_async_remote_copy(src_ref=src, dst_ref=dst, send_sem=ssem, recv_sem=rsem,
                                     device_id={"sp": peer}, device_id_type=MESH)
    c.start()
    return c


def project_kernel(h_ref, wq_ref, wk_ref, wv_ref, kc_ref, vc_ref, qs, new, cidx, ko_ref, vo_ref,
                   hbuf, wbuf, mine, recv, hsem, wsem, csem, ssem, rsem):
    me = lax.axis_index("sp")
    mate = me + 1 - 2 * lax.rem(me, 2)
    across = lax.rem(me + 2, NSP)
    qcol = pl.multiple_of(me * QW, HEAD)
    kcol = pl.multiple_of(me * HEAD, HEAD)
    hcopy = pltpu.make_async_copy(h_ref, hbuf, hsem)
    hcopy.start()
    copies = []
    for x, (lo, hi) in enumerate(PIECES):
        if hi <= QW:
            views = [(wq_ref.at[:, pl.ds(pl.multiple_of(qcol + lo, HEAD), hi - lo)], lo)]
        else:
            views = [(wk_ref.at[:, pl.ds(kcol, HEAD)], QW), (wv_ref.at[:, pl.ds(kcol, HEAD)], QW + HEAD)]
        some = []
        for y, (v, at) in enumerate(views):
            c = pltpu.make_async_copy(v, wbuf.at[:, pl.ds(at, v.shape[1])], wsem.at[x, y])
            c.start()
            some.append(c)
        copies.append(some)
    caches = []
    for j, (src, dst) in enumerate(((kc_ref, ko_ref), (vc_ref, vo_ref))):
        for i in range(2):
            part = pl.ds(i * (ROWS // 2), ROWS // 2)
            c = pltpu.make_async_copy(src.at[part], dst.at[part], csem.at[j, i])
            c.start(priority=1)
            caches.append(c)
    greet(me)
    col = lax.broadcasted_iota(jnp.int32, (32, FLAT), 1)
    head = lax.shift_right_logical(lax.broadcasted_iota(jnp.int32, (32, FLAT), 0), 3)
    cidx[...] = jnp.where(lax.bitwise_and(col, KVH - 1) == head, col, 1 << 20)
    for g in range(KVH):
        qs[pl.ds(g * 8 + GRP, ROWS, stride=32), :] = jnp.zeros((ROWS, HEAD), jnp.float32)
    hcopy.wait()
    peers = (across, NSP - 1 - me, mate)
    sends = []
    for x, (lo, hi) in enumerate(PIECES):
        for c in copies[x]:
            c.wait()
        mine[:, lo:hi] = jnp.dot(hbuf[...], wbuf[:, lo:hi], preferred_element_type=jnp.float32).astype(jnp.bfloat16)
        if x == 0:
            greeted()
        cols = pl.ds(lo, hi - lo)
        sends.append([send(mine.at[:, cols], recv.at[y, :, cols], ssem.at[x, y], rsem.at[x, y], peers[y]) for y in range(NSP - 1)])

    def place(g, x, read):
        lo, hi = PIECES[x]
        for at in range(lo, hi, HEAD):
            y = read(at).astype(jnp.float32)
            if at < QW:
                qs[pl.ds(g * 8 + at // HEAD, ROWS, stride=32), :] = y
            else:
                for r in range(4):
                    new[(at - QW) // HEAD, pl.ds(r * KVH + g, ROWS, stride=16), :] = y

    for x in range(NP):
        place(me, x, lambda at: mine[:, at:at + HEAD])
    for x in range(NP):
        for y in (2, 0, 1):
            sends[x][y].wait()
            place(peers[y], x, lambda at: recv[y, :, at:at + HEAD])
    for c in caches:
        c.wait()


def attention(first, count, unroll, rows0, len_ref, qs, cidx, k_ref, v_ref, acc, ml):
    base = lax.axis_index("sp") * SEQ
    lane = lax.broadcasted_iota(jnp.int32, (8, HEAD), 1)
    lowest = float(jnp.finfo(jnp.float32).min)

    def pair(p, carry):
        q0 = qs[pl.ds(pl.multiple_of(p * 64, 64), 32), :].astype(jnp.bfloat16)
        q1 = qs[pl.ds(pl.multiple_of(p * 64 + 32, 32), 32), :].astype(jnp.bfloat16)
        z = jnp.zeros((32, HEAD), jnp.bfloat16)
        lhs = jnp.concatenate([jnp.concatenate([q0, z], 1), jnp.concatenate([z, q1], 1)], 0)
        kk = jnp.concatenate([k_ref[2 * p], k_ref[2 * p + 1]], 1)
        s = lax.dot_general(lhs, kk, (((1,), (1,)), ((), ())), preferred_element_type=jnp.float32)
        ci = cidx[...]
        ws, ms, ls = [], [], []
        for i in range(2):
            lim = (len_ref[2 * p + i] - base) * KVH
            si = jnp.where(ci < lim, s[32 * i:32 * (i + 1)], -jnp.inf)
            m = jnp.maximum(jnp.max(si, axis=1, keepdims=True), lowest)
            w = jnp.exp2((si - m) * FACTOR)
            ls.append(jnp.sum(w, axis=1, keepdims=True))
            ms.append(m)
            ws.append(w.astype(jnp.bfloat16))
        vv = jnp.concatenate([v_ref[2 * p], v_ref[2 * p + 1]], 1)
        o = jnp.dot(jnp.concatenate(ws, 0), vv, preferred_element_type=jnp.float32)
        for i in range(2):
            b = 2 * p + i
            here = lane == b
            oi = o[32 * i:32 * (i + 1), HEAD * i:HEAD * (i + 1)]
            for g in range(KVH):
                acc[g, b - rows0] = oi[8 * g:8 * (g + 1)]
                ml[g, 0] = jnp.where(here, ms[i][8 * g:8 * (g + 1)], ml[g, 0])
                ml[g, 1] = jnp.where(here, ls[i][8 * g:8 * (g + 1)], ml[g, 1])
        return carry

    lax.fori_loop(first // 2, (first + count) // 2, pair, 0, unroll=unroll)


def attend_kernel(pos_ref, len_ref, qs, new, cidx, k_in, v_in, ko_ref, vo_ref, k_ref, v_ref, acc, ml, sem):
    del k_in, v_in
    base = lax.axis_index("sp") * SEQ
    row = lax.shift_right_logical(lax.broadcasted_iota(jnp.int32, (16, HEAD), 0), 2)

    def patch(b, carry):
        t = pos_ref[b] - base
        inside = jnp.logical_and(t >= 0, t < SEQ)
        tc = jnp.clip(t, 0, SEQ - 1)
        rows = pl.ds(pl.multiple_of(lax.shift_right_logical(tc, 2) * 16, 16), 16)
        sel = row == jnp.where(inside, lax.bitwise_and(tc, 3), -1)
        for j, ref in enumerate((k_ref, v_ref)):
            nb = new[j, pl.ds(pl.multiple_of(b * 16, 16), 16), :]
            ref[b, rows, :] = jnp.where(sel, nb, ref[b, rows, :].astype(jnp.float32)).astype(jnp.bfloat16)
        return carry

    copies = []
    for i in range(NE):
        lax.fori_loop(i * ROWS // NE, (i + 1) * ROWS // NE, patch, 0, unroll=8)
        part = pl.ds(i * (ROWS // NE), ROWS // NE)
        for j, (src, dst) in enumerate(((k_ref, ko_ref), (v_ref, vo_ref))):
            c = pltpu.make_async_copy(src.at[part], dst.at[part], sem.at[j, i])
            c.start()
            copies.append(c)
    ml[:, 0] = jnp.zeros((KVH, 8, HEAD), jnp.float32)
    ml[:, 1] = jnp.ones((KVH, 8, HEAD), jnp.float32)
    attention(0, EARLY, EARLY // 2, 0, len_ref, qs, cidx, k_ref, v_ref, acc, ml)
    for c in copies:
        c.wait()


def combine(parts):
    top = parts[0][0]
    for m, _ in parts[1:]:
        top = jnp.maximum(top, m)
    ww = [jnp.exp2((m - top) * FACTOR) for m, _ in parts]
    total = ww[0] * parts[0][1]
    for w, (_, l) in zip(ww[1:], parts[1:]):
        total = total + w * l
    return top, total, ww


def reduce_kernel(len_ref, qs, cidx, k_ref, v_ref, acc0, ml0, wo_ref, out_ref,
                  acc1, ml1, ra, rma, cross, mcross, rb, rmb, osc, attn, wbuf, part, r1, u, r2, fin, r3,
                  wsem, sa, qa, sma, qma, sb, qb, smb, qmb, s1, q1, s2, q2, s3, q3):
    me = lax.axis_index("sp")
    core = lax.rem(me, 2)
    mate = me + 1 - 2 * core
    across = lax.rem(me + 2, NSP)
    greet(me)
    wcopies = []
    for i in range(4):
        rows = pl.ds(i * (QW // 4), QW // 4)
        c = pltpu.make_async_copy(wo_ref.at[rows], wbuf.at[rows], wsem.at[i])
        c.start(priority=1)
        wcopies.append(c)
    ml1[:, 0] = jnp.zeros((KVH, 8, HEAD), jnp.float32)
    ml1[:, 1] = jnp.ones((KVH, 8, HEAD), jnp.float32)
    attention(EARLY, LATE // 2, LATE // 4, EARLY, len_ref, qs, cidx, k_ref, v_ref, acc1, ml1)
    greeted()

    theirs = (lax.rem(mate + 2, NSP), mate)
    mls = (ml0, ml1)
    accs = (acc0, acc1)
    starts = (0, EARLY)
    am, aa = {}, {}

    def to_mate(p, j, chunks):
        am[p, j] = send(mls[p].at[theirs[j]], rma.at[p, j], sma.at[p, j], qma.at[p, j], mate)
        for x in chunks:
            lo, hi = CHUNKS[x]
            aa[x, j] = send(accs[p].at[theirs[j], pl.ds(lo - starts[p], hi - lo)], ra.at[j, pl.ds(lo, hi - lo)],
                            sa.at[x, j], qa.at[x, j], mate)

    to_mate(0, 0, (0, 1))
    to_mate(0, 1, (0, 1))
    attention(EARLY + LATE // 2, LATE // 2, LATE // 4, EARLY, len_ref, qs, cidx, k_ref, v_ref, acc1, ml1)
    to_mate(1, 0, (2,))
    to_mate(1, 1, (2,))
    bm, bb = {}, {}
    for p in range(2):
        am[p, 0].wait()
        top, total, ww = combine([(mls[p][across, 0], mls[p][across, 1]), (rma[p, 0, 0], rma[p, 0, 1])])
        mcross[p, 0] = top
        mcross[p, 1] = total
        bm[p] = send(mcross.at[p], rmb.at[p], smb.at[p], qmb.at[p], across)
        for x in ((0, 1), (2,))[p]:
            lo, hi = CHUNKS[x]
            aa[x, 0].wait()
            for b in range(lo, hi):
                cross[b] = accs[p][across, b - starts[p]] * ww[0][:, b:b + 1] + ra[0, b] * ww[1][:, b:b + 1]
            rows = pl.ds(lo, hi - lo)
            bb[x] = send(cross.at[rows], rb.at[rows], sb.at[x], qb.at[x], across)
    scales = {}

    def own(p, chunks):
        if p not in scales:
            am[p, 1].wait()
            bm[p].wait()
            _, total, ww = combine([(mls[p][me, 0], mls[p][me, 1]), (rma[p, 1, 0], rma[p, 1, 1]), (rmb[p, 0], rmb[p, 1])])
            inv = 1.0 / total
            scales[p] = [w * inv for w in ww]
        scale = scales[p]
        for x in chunks:
            aa[x, 1].wait()
            bb[x].wait()
            for b in range(*CHUNKS[x]):
                osc[pl.ds(b * 8, 8), :] = (accs[p][me, b - starts[p]] * scale[0][:, b:b + 1] + ra[1, b] * scale[1][:, b:b + 1]
                                           + rb[b] * scale[2][:, b:b + 1])

    def gathered(h):
        for j in range(GRP):
            attn[h, :, j * HEAD:(j + 1) * HEAD] = osc[pl.ds(h * HR * 8 + j, HR, stride=8), :].astype(jnp.bfloat16)

    c1, c2, c3 = {}, {}, {}

    def multiply(h):
        a = attn[h]
        for k in range(NC):
            for other in (1, 0):
                half = lax.rem(core + other, 2)
                cols = pl.ds(pl.multiple_of(half * HALF + k * CC, HEAD), CC)
                part[other, h, k] = jnp.dot(a, wbuf[:, cols], preferred_element_type=jnp.float32)
                if other:
                    c1[h, k] = send(part.at[1, h, k], r1.at[h, k], s1.at[h, k], q1.at[h, k], mate)

    def pass_on(h):
        for k in range(NC):
            c1[h, k].wait()
            u[h, k] = part[0, h, k] + r1[h, k]
            c2[h, k] = send(u.at[h, k], r2.at[h, k], s2.at[h, k], q2.at[h, k], across)

    own(0, (0,))
    gathered(0)
    for c in wcopies:
        c.wait()
    multiply(0)
    own(0, (1,))
    own(1, (2,))
    gathered(1)
    pass_on(0)
    multiply(1)
    pass_on(1)
    for h in range(NH):
        for k in range(NC):
            c2[h, k].wait()
            fin[h, k] = (u[h, k] + r2[h, k]).astype(jnp.bfloat16)
            c3[h, k] = send(fin.at[h, k], r3.at[h, k], s3.at[h, k], q3.at[h, k], mate)
            out_ref[pl.ds(h * HR, HR), pl.ds(pl.multiple_of(core * HALF + k * CC, HEAD), CC)] = fin[h, k]
    for h in range(NH):
        for k in range(NC):
            c3[h, k].wait()
            out_ref[pl.ds(h * HR, HR), pl.ds(pl.multiple_of((1 - core) * HALF + k * CC, HEAD), CC)] = r3[h, k]


def solution(mesh):
    row_spec = P(('rep', 'dp'), None)
    cache_spec = P(('rep', 'dp'), 'sp', None, None)
    len_spec = P(('rep', 'dp'))
    hbm = pl.BlockSpec(memory_space=pl.ANY)
    vmem = pl.BlockSpec(memory_space=pltpu.VMEM)
    smem = pl.BlockSpec(memory_space=pltpu.SMEM)
    bf16, f32, i32 = jnp.bfloat16, jnp.float32, jnp.int32
    dma = pltpu.SemaphoreType.DMA
    shaped = jax.ShapeDtypeStruct

    def local_step(hidden, w_query, w_key, w_value, w_out, k_cache, v_cache, write_pos, valid_len):
        kc = k_cache.reshape(ROWS, FLAT, HEAD)
        vc = v_cache.reshape(ROWS, FLAT, HEAD)
        pin = lambda x: pltpu.with_memory_space_constraint(x, pltpu.HBM)
        flat = shaped((ROWS, FLAT, HEAD), bf16)
        qs, new, cidx, kv, vv = pl.pallas_call(
            project_kernel,
            out_shape=[shaped((ROWS * 32, HEAD), f32), shaped((2, ROWS * 16, HEAD), f32), shaped((32, FLAT), i32), flat, flat],
            in_specs=[hbm] * 6,
            out_specs=[vmem] * 5,
            scratch_shapes=[
                pltpu.VMEM((ROWS, DIM), bf16), pltpu.VMEM((DIM, PW), bf16),
                pltpu.VMEM((ROWS, PW), bf16), pltpu.VMEM((NSP - 1, ROWS, PW), bf16),
                dma, dma((NP, 2)), dma((2, 2)), dma((NP, NSP - 1)), dma((NP, NSP - 1))],
            compiler_params=pltpu.CompilerParams(collective_id=0, has_side_effects=True, vmem_limit_bytes=14 << 20),
            name="project",
            cost_estimate=pl.CostEstimate(flops=10_000_000_000, bytes_accessed=34_000_000, transcendentals=0),
        )(pin(hidden), pin(w_query), pin(w_key), pin(w_value), pin(kc), pin(vc))
        tiles = (8, HEAD)
        k_new, v_new, kv, vv, acc, ml = pl.pallas_call(
            attend_kernel,
            out_shape=[flat, flat, flat, flat, shaped((KVH, EARLY) + tiles, f32), shaped((KVH, 2) + tiles, f32)],
            in_specs=[smem, smem] + [vmem] * 5,
            out_specs=[hbm, hbm, vmem, vmem, vmem, vmem],
            scratch_shapes=[dma((2, NE))],
            input_output_aliases={5: 2, 6: 3},
            compiler_params=pltpu.CompilerParams(vmem_limit_bytes=4 << 20),
            name="attend",
            cost_estimate=pl.CostEstimate(flops=7_000_000_000, bytes_accessed=34_000_000, transcendentals=0),
        )(write_pos, valid_len, qs, new, cidx, kv, vv)
        parts = (NH, NC, HR, CC)
        nx = len(CHUNKS)
        attn_out = pl.pallas_call(
            reduce_kernel,
            out_shape=shaped((ROWS, DIM), bf16),
            in_specs=[smem] + [vmem] * 6 + [hbm],
            out_specs=vmem,
            scratch_shapes=[
                pltpu.VMEM((KVH, LATE) + tiles, f32), pltpu.VMEM((KVH, 2) + tiles, f32),
                pltpu.VMEM((2, ROWS) + tiles, f32), pltpu.VMEM((2, 2, 2) + tiles, f32),
                pltpu.VMEM((ROWS,) + tiles, f32), pltpu.VMEM((2, 2) + tiles, f32),
                pltpu.VMEM((ROWS,) + tiles, f32), pltpu.VMEM((2, 2) + tiles, f32),
                pltpu.VMEM((ROWS * 8, HEAD), f32), pltpu.VMEM((NH, HR, QW), bf16), pltpu.VMEM((QW, DIM), bf16),
                pltpu.VMEM((2,) + parts, f32), pltpu.VMEM(parts, f32), pltpu.VMEM(parts, f32), pltpu.VMEM(parts, f32),
                pltpu.VMEM(parts, bf16), pltpu.VMEM(parts, bf16),
                dma((4,)), dma((nx, 2)), dma((nx, 2)), dma((2, 2)), dma((2, 2)), dma((nx,)), dma((nx,)), dma((2,)), dma((2,))]
                + [dma((NH, NC))] * 6,
            compiler_params=pltpu.CompilerParams(collective_id=1, has_side_effects=True, vmem_limit_bytes=14 << 20),
            name="reduce",
            cost_estimate=pl.CostEstimate(flops=20_000_000_000, bytes_accessed=10_000_000, transcendentals=0),
        )(valid_len, qs, cidx, kv, vv, acc, ml, pin(w_out))
        shape = (ROWS, SEQ, KVH, HEAD)
        return attn_out, k_new.reshape(shape), v_new.reshape(shape)

    return jax.shard_map(local_step, mesh=mesh, in_specs=(row_spec, P(), P(), P(), P('sp', None), cache_spec, cache_spec, len_spec, len_spec), out_specs=(row_spec, cache_spec, cache_spec), check_vma=False)
```

time: 38.5 us -> 37 us (0.961)
  local copies, waits for them, and re-layouts: 1.63 us -> 0.7 us
  Pallas kernels: 36 us -> 35.4 us
    unnamed x7 -> x5, local copies, waits for them, and re-layouts: 1.63 us -> 0.7 us
    pallas_call x3, Pallas kernels: 36 us -> 35.4 us  [the longest x1 16.8 us: local_step(): pl.pallas_call(reduce_kernel, out_shape=shaped((ROWS, DIM), bf16), in_spe...]
where the time goes in v3:
time: 37 us; the launch traced here: 36.8 us
  Pallas kernels  35.4 us (96%)
  local copies, waits for them, and re-layouts  0.7 us (2%)
  between operations  0.69 us (2%)
    pallas_call x1, Pallas kernels, local_step(): pl.pallas_call(reduce_kernel, out_shape=shaped((ROWS, DIM), bf16), in_spe...  16.8 us
    pallas_call x1, Pallas kernels, local_step(): pl.pallas_call(project_kernel, out_shape=[shaped((ROWS * 32, HEAD), f32),...  11.5 us
    pallas_call x1, Pallas kernels, local_step(): pl.pallas_call(attend_kernel, out_shape=[flat, flat, flat, flat, shaped((...  7.13 us

profile of v3, /device:TPU:0, one launch (start us, length us, event | category | flops | bytes accessed | tf_op | source)
XLA Modules:
  0.0 36.8 jit_solution(383116266931159345)
XLA Ops:
  0.6 0.0 copy-start
  0.6 0.0 copy-start.1
  0.7 11.5 %project.1 = (f32[1024,128]{1,0:T(8,128)S(1)}, f32[2,512,128]{2,1,0:T(8,128)S(1)}, s32[32,1024]{1,0:T(8,128)S(1)}, bf16[32,1024,128]{2,1,0:T(8,128)(2,1)S(1)}, bf16[32,1024,128]{2,1,0:T(8,128)(2,1)S(1)}) custom-call(bf16[32,3584]{1,0:T(8,128)(2,1)} %h_ref.1, bf16[3584,3584]{1,0:T(8,128)(2,1)} %wq_ref.1, bf16[3584,512]{1,0:T(8,128)(2,1)} %wk_ref.1, ...), custom_call_target="tpu_custom_call" | custom-call | flops 10000000000 | bytes 34000000 | tf_op jit(solution)/shard_map/project/pallas_call | solution.py:325
  12.1 0.0 copy-done
  12.1 0.0 copy-done.1
  12.2 7.1 %attend.1 = (bf16[32,1024,128]{2,1,0:T(8,128)(2,1)}, bf16[32,1024,128]{2,1,0:T(8,128)(2,1)}, bf16[32,1024,128]{2,1,0:T(8,128)(2,1)S(1)}, bf16[32,1024,128]{2,1,0...) custom-call(s32[32]{0:T(128)S(1)} %copy-done, ...), custom_call_target="tpu_custom_call", output_to_operand_aliasing={{2}: (5, {}), {3}: (6, {})} | custom-call | flops 7000000000 | bytes 34000000 | tf_op jit(solution)/shard_map/attend/pallas_call | solution.py:339
  19.3 16.8 %reduce.1 = bf16[32,3584]{1,0:T(8,128)(2,1)S(1)} custom-call(s32[32]{0:T(128)S(1)} %copy-done.1, f32[1024,128]{1,0:T(8,128)S(1)} %get-tuple-element.14.qs, s32[32,1024]{1,0:T(8,128)S(1)} %get-tuple-element.15.cidx, bf16[32,1024,128]{2,1,0:T(8,128)(2,1)S(1)} %get-tuple-element.19.k_ref, bf16[32,1024,128]{2,1,0:T(8,128)(2,1)S(1)} %get-tuple-element.20.v_ref, ...), custom_call_target="tpu_custom_call" | custom-call | flops 20000000000 | bytes 10000000 | tf_op jit(solution)/shard_map/reduce/pallas_call | solution.py:352
  36.1 0.7 %copy.17 = bf16[32,3584]{1,0:T(8,128)(2,1)} copy(bf16[32,3584]{1,0:T(8,128)(2,1)S(1)} %reduce.1) | data formatting | bytes 458752
Async XLA Ops:
  0.6 11.5 %copy-start = (s32[32]{0:T(128)S(1)}, s32[32]{0:T(128)}, u32[]{:S(2)}) copy-start(s32[32]{0:T(128)} %pos_ref.1) | copy-start | bytes 388
  0.6 11.5 %copy-start.1 = (s32[32]{0:T(128)S(1)}, s32[32]{0:T(128)}, u32[]{:S(2)}) copy-start(s32[32]{0:T(128)} %len_ref.3) | copy-start | bytes 388

commit v4 on v3

--- a/solution.py
+++ b/solution.py
@@ -19,14 +19,16 @@
 PW = QW + 2 * HEAD
 PIECES = ((0, 256), (256, 512), (512, 768), (768, QW), (QW, PW))
 NP = len(PIECES)
-NE = 4
+OUT = (0, 8, 16, 24, 28, ROWS)
+NE = len(OUT) - 1
 EARLY = 24
 LATE = ROWS - EARLY
 NH = 2
 HR = ROWS // NH
 HALF = DIM // 2
-NC = 2
-CC = HALF // NC
+CUTS = ((0, 512), (512, 1280), (1280, HALF))
+NC = len(CUTS)
+LAST = (NH - 1, NC - 1)
 FACTOR = HEAD ** -0.5 * LOG2E
 CHUNKS = ((0, HR), (HR, EARLY), (EARLY, ROWS))
 
@@ -156,21 +158,26 @@
     base = lax.axis_index("sp") * SEQ
     row = lax.shift_right_logical(lax.broadcasted_iota(jnp.int32, (16, HEAD), 0), 2)
 
-    def patch(b, carry):
-        t = pos_ref[b] - base
-        inside = jnp.logical_and(t >= 0, t < SEQ)
-        tc = jnp.clip(t, 0, SEQ - 1)
-        rows = pl.ds(pl.multiple_of(lax.shift_right_logical(tc, 2) * 16, 16), 16)
-        sel = row == jnp.where(inside, lax.bitwise_and(tc, 3), -1)
-        for j, ref in enumerate((k_ref, v_ref)):
-            nb = new[j, pl.ds(pl.multiple_of(b * 16, 16), 16), :]
-            ref[b, rows, :] = jnp.where(sel, nb, ref[b, rows, :].astype(jnp.float32)).astype(jnp.bfloat16)
-        return carry
+    def patch(first, last):
+        todo = []
+        for b in range(first, last):
+            t = pos_ref[b] - base
+            inside = jnp.logical_and(t >= 0, t < SEQ)
+            tc = jnp.clip(t, 0, SEQ - 1)
+            rows = pl.ds(pl.multiple_of(lax.shift_right_logical(tc, 2) * 16, 16), 16)
+            sel = row == jnp.where(inside, lax.bitwise_and(tc, 3), -1)
+            for j, ref in enumerate((k_ref, v_ref)):
+                old = ref[b, rows, :].astype(jnp.float32)
+                todo.append((ref, b, rows, jnp.where(sel, new[j, b * 16:(b + 1) * 16, :], old).astype(jnp.bfloat16)))
+        for ref, b, rows, x in todo:
+            ref[b, rows, :] = x
 
     copies = []
     for i in range(NE):
-        lax.fori_loop(i * ROWS // NE, (i + 1) * ROWS // NE, patch, 0, unroll=8)
-        part = pl.ds(i * (ROWS // NE), ROWS // NE)
+        lo, hi = OUT[i], OUT[i + 1]
+        for b in range(lo, hi, 4):
+            patch(b, b + 4)
+        part = pl.ds(lo, hi - lo)
         for j, (src, dst) in enumerate(((k_ref, ko_ref), (v_ref, vo_ref))):
             c = pltpu.make_async_copy(src.at[part], dst.at[part], sem.at[j, i])
             c.start()
@@ -195,7 +202,7 @@
 
 def reduce_kernel(len_ref, qs, cidx, k_ref, v_ref, acc0, ml0, wo_ref, out_ref,
                   acc1, ml1, ra, rma, cross, mcross, rb, rmb, osc, attn, wbuf, part, r1, u, r2, fin, r3,
-                  wsem, sa, qa, sma, qma, sb, qb, smb, qmb, s1, q1, s2, q2, s3, q3):
+                  wsem, sa, qa, sma, qma, sb, qb, smb, qmb, s1, q1, s2, q2, s3, q3, v1, v2, sv, qv):
     me = lax.axis_index("sp")
     core = lax.rem(me, 2)
     mate = me + 1 - 2 * core
@@ -256,54 +263,72 @@
         scale = scales[p]
         for x in chunks:
             aa[x, 1].wait()
+            for b in range(*CHUNKS[x]):
+                osc[pl.ds(b * 8, 8), :] = accs[p][me, b - starts[p]] * scale[0][:, b:b + 1] + ra[1, b] * scale[1][:, b:b + 1]
+
+    def far(p, chunks):
+        for x in chunks:
             bb[x].wait()
             for b in range(*CHUNKS[x]):
-                osc[pl.ds(b * 8, 8), :] = (accs[p][me, b - starts[p]] * scale[0][:, b:b + 1] + ra[1, b] * scale[1][:, b:b + 1]
-                                           + rb[b] * scale[2][:, b:b + 1])
+                osc[pl.ds(b * 8, 8), :] += rb[b] * scales[p][2][:, b:b + 1]
 
     def gathered(h):
         for j in range(GRP):
             attn[h, :, j * HEAD:(j + 1) * HEAD] = osc[pl.ds(h * HR * 8 + j, HR, stride=8), :].astype(jnp.bfloat16)
 
-    c1, c2, c3 = {}, {}, {}
-
-    def multiply(h):
-        a = attn[h]
-        for k in range(NC):
-            for other in (1, 0):
-                half = lax.rem(core + other, 2)
-                cols = pl.ds(pl.multiple_of(half * HALF + k * CC, HEAD), CC)
-                part[other, h, k] = jnp.dot(a, wbuf[:, cols], preferred_element_type=jnp.float32)
-                if other:
-                    c1[h, k] = send(part.at[1, h, k], r1.at[h, k], s1.at[h, k], q1.at[h, k], mate)
-
-    def pass_on(h):
-        for k in range(NC):
+    c1, c2, c3, direct = {}, {}, {}, []
+    rows_of = lambda h: pl.ds(h * HR, HR)
+
+    def multiply(h, k, other):
+        lo, hi = CUTS[k]
+        half = lax.rem(core + other, 2)
+        cols = pl.ds(pl.multiple_of(half * HALF + lo, HEAD), hi - lo)
+        part[other, h, :, lo:hi] = jnp.dot(attn[h], wbuf[:, cols], preferred_element_type=jnp.float32)
+
+    def product(h):
+        for k, (lo, hi) in enumerate(CUTS):
+            multiply(h, k, 1)
+            cols = pl.ds(lo, hi - lo)
+            c1[h, k] = send(part.at[1, h, :, cols], r1.at[h, :, cols], s1.at[h, k], q1.at[h, k], mate)
+        for k, (lo, hi) in enumerate(CUTS):
+            multiply(h, k, 0)
+            cols = pl.ds(lo, hi - lo)
             c1[h, k].wait()
-            u[h, k] = part[0, h, k] + r1[h, k]
-            c2[h, k] = send(u.at[h, k], r2.at[h, k], s2.at[h, k], q2.at[h, k], across)
-
-    own(0, (0,))
-    gathered(0)
+            u[h, :, lo:hi] = part[0, h, :, lo:hi] + r1[h, :, lo:hi]
+            c2[h, k] = send(u.at[h, :, cols], r2.at[h, :, cols], s2.at[h, k], q2.at[h, k], across)
+            if (h, k) == LAST:
+                direct.append(send(u.at[h, :, cols], v1, sv.at[0], qv.at[0], mate))
+                direct.append(send(u.at[h, :, cols], v2, sv.at[1], qv.at[1], NSP - 1 - me))
+
+    own(0, (0, 1))
     for c in wcopies:
         c.wait()
-    multiply(0)
-    own(0, (1,))
+    far(0, (0,))
+    gathered(0)
+    product(0)
     own(1, (2,))
+    far(0, (1,))
+    far(1, (2,))
     gathered(1)
-    pass_on(0)
-    multiply(1)
-    pass_on(1)
+    product(1)
     for h in range(NH):
-        for k in range(NC):
+        for k, (lo, hi) in enumerate(CUTS):
             c2[h, k].wait()
-            fin[h, k] = (u[h, k] + r2[h, k]).astype(jnp.bfloat16)
-            c3[h, k] = send(fin.at[h, k], r3.at[h, k], s3.at[h, k], q3.at[h, k], mate)
-            out_ref[pl.ds(h * HR, HR), pl.ds(pl.multiple_of(core * HALF + k * CC, HEAD), CC)] = fin[h, k]
+            fin[h, :, lo:hi] = (u[h, :, lo:hi] + r2[h, :, lo:hi]).astype(jnp.bfloat16)
+            cols = pl.ds(lo, hi - lo)
+            if (h, k) != LAST:
+                c3[h, k] = send(fin.at[h, :, cols], r3.at[h, :, cols], s3.at[h, k], q3.at[h, k], mate)
+            out_ref[rows_of(h), pl.ds(pl.multiple_of(core * HALF + lo, HEAD), hi - lo)] = fin[h, :, lo:hi]
     for h in range(NH):
-        for k in range(NC):
-            c3[h, k].wait()
-            out_ref[pl.ds(h * HR, HR), pl.ds(pl.multiple_of((1 - core) * HALF + k * CC, HEAD), CC)] = r3[h, k]
+        for k, (lo, hi) in enumerate(CUTS):
+            cols = pl.ds(pl.multiple_of((1 - core) * HALF + lo, HEAD), hi - lo)
+            if (h, k) == LAST:
+                for c in direct:
+                    c.wait()
+                out_ref[rows_of(h), cols] = (v1[...] + v2[...]).astype(jnp.bfloat16)
+            else:
+                c3[h, k].wait()
+                out_ref[rows_of(h), cols] = r3[h, :, lo:hi]
 
 
 def solution(mesh):
@@ -347,7 +372,7 @@
             name="attend",
             cost_estimate=pl.CostEstimate(flops=7_000_000_000, bytes_accessed=34_000_000, transcendentals=0),
         )(write_pos, valid_len, qs, new, cidx, kv, vv)
-        parts = (NH, NC, HR, CC)
+        parts = (NH, HR, HALF)
         nx = len(CHUNKS)
         attn_out = pl.pallas_call(
             reduce_kernel,
@@ -363,7 +388,8 @@
                 pltpu.VMEM((2,) + parts, f32), pltpu.VMEM(parts, f32), pltpu.VMEM(parts, f32), pltpu.VMEM(parts, f32),
                 pltpu.VMEM(parts, bf16), pltpu.VMEM(parts, bf16),
                 dma((4,)), dma((nx, 2)), dma((nx, 2)), dma((2, 2)), dma((2, 2)), dma((nx,)), dma((nx,)), dma((2,)), dma((2,))]
-                + [dma((NH, NC))] * 6,
+                + [dma((NH, NC))] * 6
+                + [pltpu.VMEM((HR, CUTS[-1][1] - CUTS[-1][0]), f32)] * 2 + [dma((2,))] * 2,
             compiler_params=pltpu.CompilerParams(collective_id=1, has_side_effects=True, vmem_limit_bytes=14 << 20),
             name="reduce",
             cost_estimate=pl.CostEstimate(flops=20_000_000_000, bytes_accessed=10_000_000, transcendentals=0),

time: 37 us -> 36 us (0.973)
  Pallas kernels: 35.4 us -> 34.5 us
    pallas_call x1, Pallas kernels: 7.13 us -> 6.5 us  [local_step(): pl.pallas_call(attend_kernel, out_shape=[flat, flat, flat, flat, shaped((...]
where the time goes in v4:
time: 36 us; the launch traced here: 35.9 us
  Pallas kernels  34.5 us (96%)
  local copies, waits for them, and re-layouts  0.7 us (2%)
  between operations  0.69 us (2%)
    pallas_call x1, Pallas kernels, local_step(): pl.pallas_call(reduce_kernel, out_shape=shaped((ROWS, DIM), bf16), in_spe...  16.5 us
    pallas_call x1, Pallas kernels, local_step(): pl.pallas_call(project_kernel, out_shape=[shaped((ROWS * 32, HEAD), f32),...  11.5 us
    pallas_call x1, Pallas kernels, local_step(): pl.pallas_call(attend_kernel, out_shape=[flat, flat, flat, flat, shaped((...  6.5 us

profile of v4, /device:TPU:0, one launch (start us, length us, event | category | flops | bytes accessed | tf_op | source)
XLA Modules:
  0.0 35.9 jit_solution(5303138952947189339)
XLA Ops:
  0.6 0.0 copy-start
  0.6 0.0 copy-start.1
  0.7 11.5 %project.1 = (f32[1024,128]{1,0:T(8,128)S(1)}, f32[2,512,128]{2,1,0:T(8,128)S(1)}, s32[32,1024]{1,0:T(8,128)S(1)}, bf16[32,1024,128]{2,1,0:T(8,128)(2,1)S(1)}, bf16[32,1024,128]{2,1,0:T(8,128)(2,1)S(1)}) custom-call(bf16[32,3584]{1,0:T(8,128)(2,1)} %h_ref.1, bf16[3584,3584]{1,0:T(8,128)(2,1)} %wq_ref.1, bf16[3584,512]{1,0:T(8,128)(2,1)} %wk_ref.1, ...), custom_call_target="tpu_custom_call" | custom-call | flops 10000000000 | bytes 34000000 | tf_op jit(solution)/shard_map/project/pallas_call | solution.py:350
  12.1 0.0 copy-done
  12.1 0.0 copy-done.1
  12.2 6.5 %attend.1 = (bf16[32,1024,128]{2,1,0:T(8,128)(2,1)}, bf16[32,1024,128]{2,1,0:T(8,128)(2,1)}, bf16[32,1024,128]{2,1,0:T(8,128)(2,1)S(1)}, bf16[32,1024,128]{2,1,0...) custom-call(s32[32]{0:T(128)S(1)} %copy-done, ...), custom_call_target="tpu_custom_call", output_to_operand_aliasing={{2}: (5, {}), {3}: (6, {})} | custom-call | flops 7000000000 | bytes 34000000 | tf_op jit(solution)/shard_map/attend/pallas_call | solution.py:364
  18.7 16.5 %reduce.1 = bf16[32,3584]{1,0:T(8,128)(2,1)S(1)} custom-call(s32[32]{0:T(128)S(1)} %copy-done.1, f32[1024,128]{1,0:T(8,128)S(1)} %get-tuple-element.14.qs, s32[32,1024]{1,0:T(8,128)S(1)} %get-tuple-element.15.cidx, bf16[32,1024,128]{2,1,0:T(8,128)(2,1)S(1)} %get-tuple-element.19.k_ref, bf16[32,1024,128]{2,1,0:T(8,128)(2,1)S(1)} %get-tuple-element.20.v_ref, ...), custom_call_target="tpu_custom_call" | custom-call | flops 20000000000 | bytes 10000000 | tf_op jit(solution)/shard_map/reduce/pallas_call | solution.py:377
  35.2 0.7 %copy.17 = bf16[32,3584]{1,0:T(8,128)(2,1)} copy(bf16[32,3584]{1,0:T(8,128)(2,1)S(1)} %reduce.1) | data formatting | bytes 458752
Async XLA Ops:
  0.6 11.5 %copy-start = (s32[32]{0:T(128)S(1)}, s32[32]{0:T(128)}, u32[]{:S(2)}) copy-start(s32[32]{0:T(128)} %pos_ref.1) | copy-start | bytes 388
  0.6 11.5 %copy-start.1 = (s32[32]{0:T(128)S(1)}, s32[32]{0:T(128)}, u32[]{:S(2)}) copy-start(s32[32]{0:T(128)} %len_ref.3) | copy-start | bytes 388

commit v5 on v4

--- a/solution.py
+++ b/solution.py
@@ -216,7 +216,6 @@
         wcopies.append(c)
     ml1[:, 0] = jnp.zeros((KVH, 8, HEAD), jnp.float32)
     ml1[:, 1] = jnp.ones((KVH, 8, HEAD), jnp.float32)
-    attention(EARLY, LATE // 2, LATE // 4, EARLY, len_ref, qs, cidx, k_ref, v_ref, acc1, ml1)
     greeted()
 
     theirs = (lax.rem(mate + 2, NSP), mate)
@@ -234,11 +233,13 @@
 
     to_mate(0, 0, (0, 1))
     to_mate(0, 1, (0, 1))
-    attention(EARLY + LATE // 2, LATE // 2, LATE // 4, EARLY, len_ref, qs, cidx, k_ref, v_ref, acc1, ml1)
-    to_mate(1, 0, (2,))
-    to_mate(1, 1, (2,))
+    attention(EARLY, LATE // 2, LATE // 4, EARLY, len_ref, qs, cidx, k_ref, v_ref, acc1, ml1)
     bm, bb = {}, {}
     for p in range(2):
+        if p == 1:
+            attention(EARLY + LATE // 2, LATE // 2, LATE // 4, EARLY, len_ref, qs, cidx, k_ref, v_ref, acc1, ml1)
+            to_mate(1, 0, (2,))
+            to_mate(1, 1, (2,))
         am[p, 0].wait()
         top, total, ww = combine([(mls[p][across, 0], mls[p][across, 1]), (rma[p, 0, 0], rma[p, 0, 1])])
         mcross[p, 0] = top

time: 36 us -> 35.2 us (0.978)
  Pallas kernels: 34.5 us -> 33.7 us
    pallas_call x1, Pallas kernels: 16.5 us -> 15.7 us  [local_step(): pl.pallas_call(reduce_kernel, out_shape=shaped((ROWS, DIM), bf16), in_spe...]
where the time goes in v5:
time: 35.2 us; the launch traced here: 35.1 us
  Pallas kernels  33.7 us (96%)
  local copies, waits for them, and re-layouts  0.7 us (2%)
  between operations  0.69 us (2%)
    pallas_call x1, Pallas kernels, local_step(): pl.pallas_call(reduce_kernel, out_shape=shaped((ROWS, DIM), bf16), in_spe...  15.7 us
    pallas_call x1, Pallas kernels, local_step(): pl.pallas_call(project_kernel, out_shape=[shaped((ROWS * 32, HEAD), f32),...  11.5 us
    pallas_call x1, Pallas kernels, local_step(): pl.pallas_call(attend_kernel, out_shape=[flat, flat, flat, flat, shaped((...  6.5 us

profile of v5, /device:TPU:0, one launch (start us, length us, event | category | flops | bytes accessed | tf_op | source)
XLA Modules:
  0.0 35.1 jit_solution(6954759314043876993)
XLA Ops:
  0.6 0.0 copy-start
  0.6 0.0 copy-start.1
  0.7 11.5 %project.1 = (f32[1024,128]{1,0:T(8,128)S(1)}, f32[2,512,128]{2,1,0:T(8,128)S(1)}, s32[32,1024]{1,0:T(8,128)S(1)}, bf16[32,1024,128]{2,1,0:T(8,128)(2,1)S(1)}, bf16[32,1024,128]{2,1,0:T(8,128)(2,1)S(1)}) custom-call(bf16[32,3584]{1,0:T(8,128)(2,1)} %h_ref.1, bf16[3584,3584]{1,0:T(8,128)(2,1)} %wq_ref.1, bf16[3584,512]{1,0:T(8,128)(2,1)} %wk_ref.1, ...), custom_call_target="tpu_custom_call" | custom-call | flops 10000000000 | bytes 34000000 | tf_op jit(solution)/shard_map/project/pallas_call | solution.py:351
  12.1 0.0 copy-done
  12.1 0.0 copy-done.1
  12.2 6.5 %attend.1 = (bf16[32,1024,128]{2,1,0:T(8,128)(2,1)}, bf16[32,1024,128]{2,1,0:T(8,128)(2,1)}, bf16[32,1024,128]{2,1,0:T(8,128)(2,1)S(1)}, bf16[32,1024,128]{2,1,0...) custom-call(s32[32]{0:T(128)S(1)} %copy-done, ...), custom_call_target="tpu_custom_call", output_to_operand_aliasing={{2}: (5, {}), {3}: (6, {})} | custom-call | flops 7000000000 | bytes 34000000 | tf_op jit(solution)/shard_map/attend/pallas_call | solution.py:365
  18.7 15.7 %reduce.1 = bf16[32,3584]{1,0:T(8,128)(2,1)S(1)} custom-call(s32[32]{0:T(128)S(1)} %copy-done.1, f32[1024,128]{1,0:T(8,128)S(1)} %get-tuple-element.14.qs, s32[32,1024]{1,0:T(8,128)S(1)} %get-tuple-element.15.cidx, bf16[32,1024,128]{2,1,0:T(8,128)(2,1)S(1)} %get-tuple-element.19.k_ref, bf16[32,1024,128]{2,1,0:T(8,128)(2,1)S(1)} %get-tuple-element.20.v_ref, ...), custom_call_target="tpu_custom_call" | custom-call | flops 20000000000 | bytes 10000000 | tf_op jit(solution)/shard_map/reduce/pallas_call | solution.py:378
  34.4 0.7 %copy.17 = bf16[32,3584]{1,0:T(8,128)(2,1)} copy(bf16[32,3584]{1,0:T(8,128)(2,1)S(1)} %reduce.1) | data formatting | bytes 458752
Async XLA Ops:
  0.6 11.5 %copy-start = (s32[32]{0:T(128)S(1)}, s32[32]{0:T(128)}, u32[]{:S(2)}) copy-start(s32[32]{0:T(128)} %pos_ref.1) | copy-start | bytes 388
  0.6 11.5 %copy-start.1 = (s32[32]{0:T(128)S(1)}, s32[32]{0:T(128)}, u32[]{:S(2)}) copy-start(s32[32]{0:T(128)} %len_ref.3) | copy-start | bytes 388
